TPU v7x, 8 devices: a whole 2x2x1 slice. The times are simulated.
8 devices in a mesh: rep: 1 (over z), data: 2 (over y), expert: 4 (over x, core).
Axes of the slice: x: 2, y: 2, z: 1, core: 2. Of those that a mesh axis runs over, the one named last changes fastest.
Arguments:
- x: bfloat16 [32768, 2048], P(('rep', 'expert', 'data'))
- expert_idx: int32 [32768, 2], P(('rep', 'expert', 'data'))
- gate: float32 [32768, 2], P(('rep', 'expert', 'data'))
- w_gate: bfloat16 [8, 2048, 5632], P('expert', 'data')
- w_up: bfloat16 [8, 2048, 5632], P('expert', 'data')
- w_down: bfloat16 [8, 5632, 2048], P('expert', None, 'data')
Outputs:
- output: bfloat16 [32768, 2048], P(('rep', 'expert', 'data'))
All inputs are finite; a program needn't handle non-finite values.
Results may differ from a plain program's by a relative error of at most 0.001.
Values are sent between devices in bfloat16 or wider.
A program may use at most 1 GiB of HBM per device.

v0:
```python
import functools

import jax
import jax.numpy as jnp
from jax import lax
from jax.experimental import pallas as pl
from jax.experimental.pallas import tpu as pltpu
from jax.sharding import PartitionSpec as P


BF16 = jnp.bfloat16
F32 = jnp.float32
I32 = jnp.int32
VMEM_LIMIT = 66_000_000

TILE = 256
TOK_BLOCK = 256
MIX_TILE = 128
ALIGN = 16
REACH = 512
DOWN_BLOCK = 512
SUB = 512
WIDE_CHUNKS = (512, 2048, 1536, 1536)
DOWN_PIECES = ((0, 0, 512), (1, 0, 512), (0, 512, 256), (1, 512, 256), (0, 768, 256), (1, 768, 128), (1, 896, 128))


def capacity_rows(tok_rows, top_k, n_exp):
    return max(8, ((5 * top_k * tok_rows) // (4 * n_exp) + 7) // 8 * 8)


def after(value, *earlier):
    return lax.optimization_barrier((value, earlier))[0]


def any_spec():
    return pl.BlockSpec(memory_space=pl.ANY)


def pack_body(n_local, local, n_blk, n_group, first_ref, slot_ref, x_ref, *refs):
    out_refs, acc_ref = refs[:n_group], refs[n_group]
    e, s = pl.program_id(0) * n_local + local, pl.program_id(1)
    count = first_ref[e * (n_blk + 1) + n_blk]
    base = s * TILE

    @pl.when(base < count)
    def _():
        end = jnp.minimum(base + TILE, count)
        lo = jnp.int32(0)
        hi = jnp.int32(0)
        for i in range(n_blk):
            lo += (first_ref[e * (n_blk + 1) + i + 1] <= base).astype(I32)
            hi += (first_ref[e * (n_blk + 1) + i] < end).astype(I32)
        acc_ref[...] = jnp.zeros_like(acc_ref)
        slots = base + lax.broadcasted_iota(I32, (TILE, TOK_BLOCK), 0)

        def visit(i, carry):
            off = pl.multiple_of(i * TOK_BLOCK, TOK_BLOCK)
            pick = (slots == slot_ref[pl.ds(e, 1), pl.ds(off, TOK_BLOCK)]).astype(F32).astype(BF16)
            acc_ref[...] += jnp.dot(pick, x_ref[pl.ds(off, TOK_BLOCK), :], preferred_element_type=F32)
            return carry

        lax.fori_loop(lo, hi, visit, 0)
        for d in range(n_group):

            @pl.when(pl.program_id(0) == d)
            def _():
                out_refs[d][...] = acc_ref[...].astype(BF16)


def pack_rows(first_blk, x_loc, slot_te, n_exp, n_local, local, capacity):
    tok_rows, d_model = x_loc.shape
    n_blk = tok_rows // TOK_BLOCK
    n_group = n_exp // n_local

    def out_spec(d):
        def index(p, s, first):
            used = (first[(d * n_local + local) * (n_blk + 1) + n_blk] + TILE - 1) // TILE
            last = jnp.maximum(used - 1, 0)
            return jnp.where(p < d, 0, jnp.where(p > d, last, jnp.minimum(s, last))), 0

        return pl.BlockSpec((TILE, d_model), index)

    return pl.pallas_call(
        functools.partial(pack_body, n_local, local, n_blk, n_group),
        grid_spec=pltpu.PrefetchScalarGridSpec(
            num_scalar_prefetch=1,
            grid=(n_group, capacity // TILE),
            in_specs=[
                pl.BlockSpec((n_exp, tok_rows), lambda p, s, f: (0, 0)),
                pl.BlockSpec((tok_rows, d_model), lambda p, s, f: (0, 0)),
            ],
            out_specs=[out_spec(d) for d in range(n_group)],
            scratch_shapes=[pltpu.VMEM((TILE, d_model), F32)],
        ),
        out_shape=[jax.ShapeDtypeStruct((capacity, d_model), BF16)] * n_group,
        compiler_params=pltpu.CompilerParams(vmem_limit_bytes=VMEM_LIMIT),
        cost_estimate=pl.CostEstimate(flops=20_000_000_000, bytes_accessed=60_000_000, transcendentals=0),
        name="pack_rows",
    )(first_blk, slot_te, x_loc)


def smem():
    return pl.BlockSpec(memory_space=pltpu.SMEM)


def tile_at(i):
    return pl.ds(pl.multiple_of(i * TILE, TILE), TILE)


def wide_body(n_group, n_far, local, lo_col, cols, meta_ref, *refs):
    x_refs = refs[:n_group]
    wg_ref, wu_ref = refs[n_group : n_group + 2]
    far_refs = refs[n_group + 2 : n_group + 2 + n_far]
    far_g, far_u = far_refs if n_far == 2 else (far_refs[0].at[0], far_refs[0].at[1])
    h_ref, rows_buf, h_buf, gate_w, up_w, row_sems, h_sems, sems = refs[-8:]
    side = meta_ref[0]
    half = wg_ref.shape[1]
    n_live = meta_ref[1 + n_group]

    def fetch(i):
        for d in range(n_group):

            @pl.when((i >= meta_ref[1 + d]) & (i < meta_ref[2 + d]))
            def _():
                pltpu.make_async_copy(x_refs[d].at[tile_at(i - meta_ref[1 + d]), :], rows_buf.at[i % 2], row_sems.at[i % 2]).start()

    def send(i):
        return pltpu.make_async_copy(h_buf.at[i % 2], h_ref.at[tile_at(i), pl.ds(lo_col, cols)], h_sems.at[i % 2])

    fetch(0)
    near = pl.ds(pl.multiple_of(side * half, half), half)
    far = pl.ds(pl.multiple_of((1 - side) * half, half), half)
    copies = [
        pltpu.make_async_copy(wg_ref.at[local, :, pl.ds(lo_col, cols)], gate_w.at[near, :], sems.at[0]),
        pltpu.make_async_copy(wu_ref.at[local, :, pl.ds(lo_col, cols)], up_w.at[near, :], sems.at[1]),
        pltpu.make_async_copy(far_g, gate_w.at[far, :], sems.at[2]),
        pltpu.make_async_copy(far_u, up_w.at[far, :], sems.at[3]),
    ]
    for copy in copies:
        copy.start()
    for copy in copies:
        copy.wait()

    def step(i, carry):
        fetch(i + 1)
        pltpu.make_async_copy(x_refs[0].at[tile_at(0), :], rows_buf.at[i % 2], row_sems.at[i % 2]).wait()

        @pl.when(i >= 2)
        def _():
            send(i - 2).wait()

        def part(j, carry):
            span = pl.ds(pl.multiple_of(j * SUB, SUB), SUB)
            rows = rows_buf[i % 2]
            g = jnp.dot(rows, gate_w[:, span], preferred_element_type=F32)
            u = jnp.dot(rows, up_w[:, span], preferred_element_type=F32)
            h_buf[i % 2, :, span] = (jax.nn.silu(g) * u).astype(BF16)
            return carry

        lax.fori_loop(0, cols // SUB, part, 0)
        send(i).start()
        return carry

    lax.fori_loop(0, n_live, step, 0)
    for back in (2, 1):

        @pl.when(n_live >= back)
        def _():
            send(n_live - back).wait()


def wide_part(meta, hidden, rows, w_gate, w_up, far, local, lo_col, cols):
    n_group = len(rows)
    capacity, d_model = rows[0].shape
    n_rows = n_group * capacity
    ffn = w_gate.shape[2]
    far = far if isinstance(far, list) else [far]
    args = [meta, *rows, w_gate, w_up, *far]
    alias = {}
    if hidden is not None:
        alias = {len(args): 0}
        args.append(hidden)
    return pl.pallas_call(
        functools.partial(wide_body, n_group, len(far), local, lo_col, cols),
        in_specs=[smem()] + [any_spec()] * (len(args) - 1),
        out_specs=any_spec(),
        scratch_shapes=[
            pltpu.VMEM((2, TILE, d_model), BF16),
            pltpu.VMEM((2, TILE, cols), BF16),
            pltpu.VMEM((d_model, cols), BF16),
            pltpu.VMEM((d_model, cols), BF16),
            pltpu.SemaphoreType.DMA((2,)),
            pltpu.SemaphoreType.DMA((2,)),
            pltpu.SemaphoreType.DMA((4,)),
        ],
        out_shape=jax.ShapeDtypeStruct((n_rows, ffn), BF16),
        input_output_aliases=alias,
        compiler_params=pltpu.CompilerParams(vmem_limit_bytes=VMEM_LIMIT),
        cost_estimate=pl.CostEstimate(flops=4 * n_rows * d_model * cols, bytes_accessed=n_rows * d_model * 2, transcendentals=0),
        name="wide_part",
    )(*args)


def down_body(segs, local, deep, pair_size, n_hidden, meta_ref, *refs):
    h_refs, w_ref, refs = refs[:n_hidden], refs[n_hidden], refs[n_hidden + 1 :]
    out_refs = refs[: len(segs)]
    h_buf, out_buf, w_buf, h_sems, out_sems, sem = refs[len(segs) :]
    begin = meta_ref[1 + segs[0]]
    n_live = meta_ref[2 + segs[-1]] - begin
    block = min(w_buf.shape[1], DOWN_BLOCK)

    def fetch(i):
        for l, h_ref in enumerate(h_refs):
            copy = pltpu.make_async_copy(h_ref.at[tile_at(begin + i), :], h_buf.at[i % deep], h_sems.at[i % deep])
            if n_hidden == 1:
                copy.start()
            else:
                pl.when(meta_ref[0] == l)(copy.start)

    def fetched(i):
        pltpu.make_async_copy(h_refs[0].at[tile_at(0), :], h_buf.at[i % deep], h_sems.at[i % deep]).wait()

    def sent(i):
        pltpu.make_async_copy(out_buf.at[i % deep], out_refs[0].at[tile_at(0), :], out_sems.at[i % deep]).wait()

    def send(i, there, tile):
        pltpu.make_async_copy(out_buf.at[i % deep], there.at[tile_at(tile), :], out_sems.at[i % deep]).start()

    copy = pltpu.make_async_copy(w_ref if local is None else w_ref.at[local], w_buf, sem)
    copy.start()
    for i in range(deep - pair_size):

        @pl.when(i < n_live)
        def _():
            fetch(i)

    copy.wait()

    def step(pair, carry):
        for k in range(pair_size):
            i = pair * pair_size + k

            @pl.when(i + deep - pair_size < n_live)
            def _():
                fetch(i + deep - pair_size)

        for k in range(pair_size):
            i = pair * pair_size + k

            @pl.when(i < n_live)
            def _():
                fetched(i)

            @pl.when((i >= deep) & (i - deep < n_live))
            def _():
                sent(i)

        slots = pl.ds(pair % (deep // pair_size) * pair_size, pair_size)

        def part(j, carry):
            span = pl.ds(pl.multiple_of(j * block, block), block)
            total = jnp.dot(h_buf[slots].reshape(pair_size * TILE, -1), w_buf[:, span], preferred_element_type=F32)
            out_buf[slots, :, span] = total.astype(BF16).reshape(pair_size, TILE, -1)
            return carry

        lax.fori_loop(0, w_buf.shape[1] // block, part, 0)
        for k in range(pair_size):
            i = pair * pair_size + k
            for d, out_ref in zip(segs, out_refs):

                @pl.when((begin + i >= meta_ref[1 + d]) & (begin + i < meta_ref[2 + d]))
                def _():
                    send(i, out_ref, begin + i - meta_ref[1 + d])

        return carry

    n_pair = (n_live + pair_size - 1) // pair_size
    lax.fori_loop(0, n_pair, step, 0)
    for back in range(deep, 0, -1):
        i = n_pair * pair_size - back

        @pl.when((i >= 0) & (i < n_live))
        def _():
            sent(i)

    for d, out_ref in zip(segs, out_refs):
        @pl.when(meta_ref[1 + d] == meta_ref[2 + d])
        def _():
            out_buf[0] = jnp.zeros_like(out_buf[0])
            send(0, out_ref, 0)
            sent(0)


def down_part(meta, hidden, weight, n_group, local=None, segs=None):
    segs = tuple(range(n_group)) if segs is None else segs
    n_rows = hidden[0].shape[0]
    n_hid, width = weight.shape[-2:]
    deep, pair_size = 4, 1
    return pl.pallas_call(
        functools.partial(down_body, segs, local, deep, pair_size, len(hidden)),
        in_specs=[smem()] + [any_spec()] * (len(hidden) + 1),
        out_specs=[any_spec()] * len(segs),
        scratch_shapes=[
            pltpu.VMEM((deep, TILE, n_hid), BF16),
            pltpu.VMEM((deep, TILE, width), BF16),
            pltpu.VMEM((n_hid, width), BF16),
            pltpu.SemaphoreType.DMA((deep,)),
            pltpu.SemaphoreType.DMA((deep,)),
            pltpu.SemaphoreType.DMA,
        ],
        out_shape=[jax.ShapeDtypeStruct((n_rows // n_group, width), BF16)] * len(segs),
        compiler_params=pltpu.CompilerParams(vmem_limit_bytes=VMEM_LIMIT),
        cost_estimate=pl.CostEstimate(flops=2 * n_rows * n_hid * width, bytes_accessed=n_rows * n_hid * 2, transcendentals=0),
        name="down_part",
    )(meta, *hidden, weight)


def mix_body(n_exp, n_tile, subs, widths, unroll, col_ref, chunk_ref, pos_ref, gate_ref, x_ref, *refs):
    n_set = len(widths)
    back_refs = refs[: n_set * n_exp]
    y_ref, mark_ref, pos_buf, gate_buf = refs[-6 - 4 * n_set : -2 - 4 * n_set]
    bufs, sems, y_sems = refs[-2 - 4 * n_set : -2], refs[-2], refs[-1]
    sets = []
    copies = [pltpu.make_async_copy(pos_ref, pos_buf, sems.at[0]), pltpu.make_async_copy(gate_ref, gate_buf, sems.at[1])]
    for g, width in enumerate(widths):
        back_buf, near_buf, x_buf, y_buf = bufs[4 * g : 4 * g + 4]
        cols = pl.ds(pl.multiple_of(col_ref[g], 128), width)
        sets.append((back_buf, near_buf, x_buf, y_buf, cols))
        for e in range(n_exp):
            ref, sub = back_refs[g * n_exp + e], subs[g * n_exp + e]
            capacity = ref.shape[0]
            here = back_buf.at[pl.ds(e * capacity, capacity), :]
            copies.append(pltpu.make_async_copy(ref.at[:, pl.ds(sub * width, width)], here, sems.at[len(copies)]))
        copies.append(pltpu.make_async_copy(x_ref.at[:, cols], x_buf, sems.at[len(copies)]))
    for copy in copies:
        copy.start()
    for copy in copies:
        copy.wait()

    def out(g, block):
        _, _, _, y_buf, cols = sets[g]
        rows = pl.ds(pl.multiple_of(block * (unroll * MIX_TILE), unroll * MIX_TILE), unroll * MIX_TILE)
        return pltpu.make_async_copy(y_buf.at[rows, :], y_ref.at[rows, cols], y_sems.at[g, block])

    def step(block, carry):
        for k in range(unroll):
            i = block * unroll + k
            tokens = pl.ds(pl.multiple_of(i * MIX_TILE, MIX_TILE), MIX_TILE)
            seat = lax.broadcasted_iota(I32, (MIX_TILE, REACH), 1)
            pick = jnp.concatenate([(seat == pos_buf[tokens, j : j + 1]).astype(F32).astype(BF16) for j in range(2)], axis=0)
            for back_buf, near_buf, x_buf, y_buf, _ in sets:
                for c in range(REACH // ALIGN):
                    chunk = pl.multiple_of(chunk_ref[i * (REACH // ALIGN) + c], ALIGN)
                    near_buf[k, c * ALIGN : (c + 1) * ALIGN, :] = back_buf[pl.ds(chunk, ALIGN), :]
                found = jnp.dot(pick, near_buf[k], preferred_element_type=F32)
                mixed = gate_buf[tokens, 0:1] * found[:MIX_TILE] + gate_buf[tokens, 1:2] * found[MIX_TILE:]
                y_buf[tokens, :] = (x_buf[tokens, :].astype(F32) + mixed).astype(BF16)
        for g in range(n_set):
            out(g, block).start()
        return carry

    lax.fori_loop(0, n_tile // unroll, step, 0)
    for block in range(n_tile // unroll):
        for g in range(n_set):
            out(g, block).wait()
    mark_ref[0] = 0


def mix_cols(col, y_loc, x_loc, pos, gate_loc, chunks, widths, back):
    tok_rows, d_model = x_loc.shape
    n_exp = len(back) // len(widths)
    capacity = back[0][0].shape[0]
    unroll = 4 if sum(widths) < 256 else 2
    args = [col, chunks, pos, gate_loc, x_loc, *[array for array, _ in back]]
    specs = [smem(), smem()] + [any_spec()] * (3 + len(back))
    alias = {}
    if y_loc is not None:
        alias = {len(args): 0}
        args.append(y_loc)
        specs.append(any_spec())
    bufs = [pltpu.VMEM(pos.shape, I32), pltpu.VMEM(gate_loc.shape, F32)]
    for width in widths:
        bufs += [
            pltpu.VMEM((n_exp * capacity, width), BF16),
            pltpu.VMEM((unroll, REACH, width), BF16),
            pltpu.VMEM((tok_rows, width), BF16),
            pltpu.VMEM((tok_rows, width), BF16),
        ]
    return pl.pallas_call(
        functools.partial(mix_body, n_exp, tok_rows // MIX_TILE, tuple(sub for _, sub in back), widths, unroll),
        in_specs=specs,
        out_specs=[any_spec(), smem()],
        scratch_shapes=bufs
        + [
            pltpu.SemaphoreType.DMA((2 + (n_exp + 1) * len(widths),)),
            pltpu.SemaphoreType.DMA((len(widths), tok_rows // MIX_TILE // unroll)),
        ],
        out_shape=[jax.ShapeDtypeStruct((tok_rows, d_model), BF16), jax.ShapeDtypeStruct((1,), I32)],
        input_output_aliases=alias,
        compiler_params=pltpu.CompilerParams(vmem_limit_bytes=VMEM_LIMIT),
        cost_estimate=pl.CostEstimate(flops=20_000_000 * sum(widths), bytes_accessed=20_000 * sum(widths), transcendentals=0),
        name="mix_cols",
    )(*args)


def spans(sizes):
    lo = 0
    for size in sizes:
        yield lo, size
        lo += size


def solution(mesh):
    n_group, n_side = mesh.shape["expert"], mesh.shape["data"]
    tok_spec = P(("rep", "expert", "data"), None)
    wide_spec = P("expert", "data", None)
    down_spec = P("expert", None, "data")
    swap = [(s, 1 - s) for s in range(n_side)]

    def whole_step(x_loc, idx_loc, gate_loc, wg_loc, wu_loc, wd_loc):
        tok_rows, _ = x_loc.shape
        top_k = idx_loc.shape[1]
        n_local, half, ffn = wg_loc.shape
        n_exp = n_local * n_group
        capacity = capacity_rows(tok_rows, top_k, n_exp)
        side = lax.axis_index("data")
        place = lax.axis_index("expert")
        locals_ = range(n_local)
        groups = jnp.arange(n_group, dtype=I32)

        ids = ((idx_loc // n_local + n_group - place) % n_group * n_local + idx_loc % n_local).T
        experts = jnp.arange(n_exp, dtype=I32)[:, None]
        chosen = functools.reduce(jnp.logical_or, [ids[j][None, :] == experts for j in range(top_k)])
        chosen_i = chosen.astype(I32)
        running = jnp.cumsum(chosen_i, axis=1)
        before = running - chosen_i
        slot_te = jnp.where(chosen & (before < capacity), before, -1)
        counts = jnp.minimum(running[:, -1], capacity)
        first = jnp.minimum(before, capacity)
        first_blk = jnp.concatenate([first[:, ::TOK_BLOCK], counts[:, None]], axis=1).reshape(-1)
        first_mix = first[:, ::MIX_TILE]

        table = lax.all_gather(counts, "expert")
        meta = []
        for l in locals_:
            mine = jnp.sum(jnp.where(((place - groups) % n_group)[:, None, None] == groups[None, :, None], table.reshape(n_group, n_group, n_local)[None, :, :, l] * (groups[:, None, None] == groups[None, None, :]), 0), axis=(1, 2))
            ends = jnp.cumsum((mine + TILE - 1) // TILE)
            meta.append(jnp.concatenate([side[None], jnp.zeros((1,), I32), ends]).astype(I32))

        reach = REACH // ALIGN
        start = first_mix // ALIGN
        stop = jnp.concatenate([first_mix[:, 1:], counts[:, None]], axis=1)
        size = jnp.where(stop > first_mix, (stop + ALIGN - 1) // ALIGN - start, 0)
        lead = jnp.cumsum(size, axis=0) - size
        at = slot_te + jnp.repeat((lead - start) * ALIGN, MIX_TILE, axis=1)
        at = jnp.where(slot_te < 0, -1, at)
        pos = jnp.stack([jnp.sum(jnp.where(ids[j][None, :] == experts, at, 0), axis=0) for j in range(top_k)], axis=1)
        seat = jnp.arange(reach, dtype=I32)[None, None, :]
        taken = (seat >= lead[:, :, None]) & (seat < (lead + size)[:, :, None])

        def chunk_table(array):
            source = array[:, :, None] * (capacity // ALIGN) + (start - lead)[:, :, None] + seat
            return (jnp.sum(jnp.where(taken, source, 0), axis=0) * ALIGN).reshape(-1)

        chunks = chunk_table(experts)

        done = []

        def in_turn(kernel, small, *args, follows=True):
            if done and follows:
                small = after(small, done[-1]) if done[-1].ndim else small + done[-1]
            out = kernel(small, *args)
            done.append(out[0] if isinstance(out, (list, tuple)) else out)
            return out

        wide_spans = list(spans(WIDE_CHUNKS))
        parts = [[w[0, :, : wide_spans[0][1]] for w in (wg_loc, wu_loc)]]
        later = after((wg_loc, wu_loc), parts[0])
        parts += [jnp.stack([w[l, :, lo : lo + n] for w in later]) for l in locals_ for lo, n in wide_spans if l or lo]
        far = []

        def cross():
            if len(far) == len(parts):
                return
            piece = parts[len(far)]
            if len(far) >= 2:
                piece = after(piece, far[-2])
            far.append(lax.ppermute(piece, "data", swap))

        def exchange(blocks, step):
            out = [blocks[0]]
            for d in range(1, n_group):
                out.append(lax.ppermute(blocks[d], "expert", [(s, (s + step * d) % n_group) for s in range(n_group)]))
            return out

        def mix(y_loc, chunks, *sets):
            col = jnp.stack([col for col, _, _ in sets]).astype(I32)
            back = [(pair[l][0][d], pair[l][1]) for _, _, pair in sets for d in range(n_group) for l in locals_]
            out = in_turn(mix_cols, col, y_loc, x_loc, pos, gate_loc, chunks, tuple(width for _, width, _ in sets), back)
            done[-1] = out[1][0]
            return out[0]

        cross()
        cross()
        first_blk = after(first_blk, meta)
        rows = [exchange(in_turn(pack_rows, first_blk, x_loc, slot_te, n_exp, n_local, 0, capacity), 1)]
        cross()
        packed = in_turn(pack_rows, first_blk, x_loc, slot_te, n_exp, n_local, 1, capacity)
        cross()
        rows.append(exchange([after(block, rows[0]) for block in packed], 1))

        n_wide = len(wide_spans)
        hidden, own = [], []
        for l in locals_:
            hidden.append(None)
            for k, (lo, n) in enumerate(wide_spans):
                if k >= 2 or (l and k):
                    cross()
                hidden[l] = in_turn(wide_part, meta[l], hidden[l], rows[l], wg_loc, wu_loc, far[l * n_wide + k], l, lo, n, follows=k == 0)
                if not (l or k):
                    at_group = (groups[:, None, None] + groups[None, :, None]) % n_group == groups[None, None, :]
                    held = table.reshape(n_group, n_group, 1, n_local)
                    totals = after(jnp.sum(jnp.where(at_group[..., None], held, 0), axis=(0, 1)), done[-1])
                    totals += lax.ppermute(totals, "data", swap)
            if l == 0:
                cross()
                flips = (totals[:, 1] > totals[:, 0]).astype(I32)
                flip = jnp.sum(jnp.where(groups == place, flips, 0))
                parts += [lax.dynamic_slice(wd_loc, ((r + flip) % n_local, 0, lo), (1, ffn, n))[0] for r, lo, n in DOWN_PIECES]
            own.append(exchange(in_turn(down_part, meta[l], [hidden[l]], wd_loc, n_group, l, follows=False), -1))

        role_meta = []
        for r in locals_:
            picked = jnp.where(flip == 1, meta[(r + 1) % n_local], meta[r])
            role_meta.append(jnp.concatenate([((r + flip) % n_local)[None], picked[1:]]))
        d_flips = jnp.sum(jnp.where(((place + groups) % n_group)[:, None] == groups[None, :], flips[None, :], 0), axis=1)
        roles = (jnp.arange(n_local, dtype=I32)[None, :] + d_flips[:, None]) % n_local
        far_chunks = chunk_table((groups[:, None] * n_local + roles).reshape(n_exp, 1))

        def far_piece(i):
            cross()
            r = DOWN_PIECES[i][0]
            return exchange(in_turn(down_part, role_meta[r], hidden, far[n_local * n_wide + i], n_group), -1)

        far_col = (1 - side) * half
        ret = [far_piece(0), far_piece(1)]
        y_loc = mix(None, chunks, (side * half, half, [(own[l], 0) for l in locals_]))
        ret += [far_piece(2), far_piece(3)]
        y_loc = mix(y_loc, far_chunks, (far_col, 512, [(ret[0], 0), (ret[1], 0)]))
        ret.append(far_piece(4))
        y_loc = mix(y_loc, far_chunks, (far_col + 512, 256, [(ret[2], 0), (ret[3], 0)]))
        ret += [far_piece(5), far_piece(6)]
        y_loc = mix(y_loc, far_chunks, (far_col + 768, 128, [(ret[4], 0), (ret[5], 0)]))
        return mix(y_loc, far_chunks, (far_col + 896, 128, [(ret[4], 1), (ret[6], 0)]))

    in_specs = (tok_spec, tok_spec, tok_spec, wide_spec, wide_spec, down_spec)
    return jax.shard_map(whole_step, mesh=mesh, in_specs=in_specs, out_specs=tok_spec, check_vma=False)
```

profile of v0, /device:TPU:0, one launch (start us, length us, event | category | flops | bytes accessed | tf_op | source)
XLA Modules:
  0.0 1903.6 jit_solution(3238069226663643187)
XLA Ops:
  6.4 6.7 all-reduce
  17.1 40.5 %pack_rows.2 = (bf16[1280,2048]{1,0:T(8,128)(2,1)}, bf16[1280,2048]{1,0:T(8,128)(2,1)}, bf16[1280,2048]{1,0:T(8,128)(2,1)}, bf16[1280,2048]{1,0:T(8,128)(2,1)}) custom-call(s32[136]{0:T(256)} %reshape.418.first_ref, s32[8,4096]{1,0:T(8,128)} %get-tuple-element.206.slot_ref, bf16[4096,2048]{1,0:T(8,128)(2,1)} %x_ref.13), custom_call_target="tpu_custom_call" | custom-call | flops 20000000000 | bytes 60000000 | tf_op jit(solution)/shard_map/pack_rows/pallas_call | solution.py:83
  66.3 11.4 fusion.28
  77.7 6.3 pad_maximum_fusion.1
  85.5 17.8 fusion.26
  116.1 45.2 %pack_rows.3 = (bf16[1280,2048]{1,0:T(8,128)(2,1)}, bf16[1280,2048]{1,0:T(8,128)(2,1)}, bf16[1280,2048]{1,0:T(8,128)(2,1)}, bf16[1280,2048]{1,0:T(8,128)(2,1)}) custom-call(s32[136]{0:T(256)} %reshape.418.first_ref, s32[8,4096]{1,0:T(8,128)} %get-tuple-element.206.slot_ref, bf16[4096,2048]{1,0:T(8,128)(2,1)} %x_ref.13), custom_call_target="tpu_custom_call" | custom-call | flops 20000000000 | bytes 60000000 | tf_op jit(solution)/shard_map/pack_rows/pallas_call | solution.py:83
  188.7 101.3 %collective-permute-done.4.refs_7_ = bf16[1024,512]{1,0:T(8,128)(2,1)} collective-permute-done((bf16[1024,512]{1,0:T(8,128)(2,1)}, bf16[1024,512]{1,0:T(8,128)(2,1)}, u32[]{:S(2)}, u32[]{:S(2)}) %collective-permute-start.4) | collective-permute-done | bytes 1048608 | tf_op jit(solution)/shard_map/ppermute | solution.py:488
  290.9 22.0 %wide_part.8.refs_7_ = bf16[5120,5632]{1,0:T(8,128)(2,1)} custom-call(s32[6]{0:T(128)} %pad_add_fusion.3.meta_ref, bf16[1280,2048]{1,0:T(8,128)(2,1)} %get-tuple-element.91.refs_0_, bf16[1280,2048]{1,0:T(8,128)(2,1)} %collective-permute-done.refs_1_, bf16[1280,2048]{1,0:T(8,128)(2,1)} %collective-permute-done.1.refs_2_, ...), custom_call_target="tpu_custom_call" | custom-call | flops 21474836480 | bytes 20971520 | tf_op jit(solution)/shard_map/wide_part/pallas_call | solution.py:183
  313.0 10.2 collective-permute-start.7
  323.2 102.8 %collective-permute-done.5 = s32[4,2]{0,1:T(2,128)S(1)} collective-permute-done((s32[4,2]{0,1:T(2,128)S(1)}, s32[4,2]{0,1:T(2,128)S(1)}, u32[]{:S(2)}, u32[]{:S(2)}) %collective-permute-start.5) | collective-permute-done | bytes 64 | tf_op jit(solution)/shard_map/ppermute | solution.py:524
  437.3 7.0 dynamic-slice_bitcast_fusion.2
  444.3 9.3 dynamic-slice_bitcast_fusion
  455.7 79.1 %wide_part.9.refs_7_ = bf16[5120,5632]{1,0:T(8,128)(2,1)} custom-call(s32[6]{0:T(128)} %pad_add_fusion.3.meta_ref, bf16[1280,2048]{1,0:T(8,128)(2,1)} %get-tuple-element.91.refs_0_, bf16[1280,2048]{1,0:T(8,128)(2,1)} %collective-permute-done.refs_1_, bf16[1280,2048]{1,0:T(8,128)(2,1)} %collective-permute-done.1.refs_2_, ...), custom_call_target="tpu_custom_call", output_to_operand_aliasing={{}: (8, {})} | custom-call | flops 85899345920 | bytes 20971520 | tf_op jit(solution)/shard_map/wide_part/pallas_call | solution.py:183
  534.9 59.5 %wide_part.10.refs_7_ = bf16[5120,5632]{1,0:T(8,128)(2,1)} custom-call(s32[6]{0:T(128)} %pad_add_fusion.3.meta_ref, bf16[1280,2048]{1,0:T(8,128)(2,1)} %get-tuple-element.91.refs_0_, bf16[1280,2048]{1,0:T(8,128)(2,1)} %collective-permute-done.refs_1_, bf16[1280,2048]{1,0:T(8,128)(2,1)} %collective-permute-done.1.refs_2_, ...), custom_call_target="tpu_custom_call", output_to_operand_aliasing={{}: (8, {})} | custom-call | flops 64424509440 | bytes 20971520 | tf_op jit(solution)/shard_map/wide_part/pallas_call | solution.py:183
  594.4 42.9 %collective-permute-done.10.refs_6_ = bf16[2,1024,1536]{2,1,0:T(8,128)(2,1)} collective-permute-done((bf16[2,1024,1536]{2,1,0:T(8,128)(2,1)}, bf16[2,1024,1536]{2,1,0:T(8,128)(2,1)}, u32[]{:S(2)}, u32[]{:S(2)}) %collective-permute-start.10) | collective-permute-done | bytes 6291488 | tf_op jit(solution)/shard_map/ppermute | solution.py:488
  638.1 59.6 %wide_part.11.refs_0_ = bf16[5120,5632]{1,0:T(8,128)(2,1)} custom-call(s32[6]{0:T(128)} %pad_add_fusion.3.meta_ref, bf16[1280,2048]{1,0:T(8,128)(2,1)} %get-tuple-element.91.refs_0_, bf16[1280,2048]{1,0:T(8,128)(2,1)} %collective-permute-done.refs_1_, bf16[1280,2048]{1,0:T(8,128)(2,1)} %collective-permute-done.1.refs_2_, ...), custom_call_target="tpu_custom_call", output_to_operand_aliasing={{}: (8, {})} | custom-call | flops 64424509440 | bytes 20971520 | tf_op jit(solution)/shard_map/wide_part/pallas_call | solution.py:183
  697.7 74.4 %collective-permute-done.15.refs_6_ = bf16[2,1024,1536]{2,1,0:T(8,128)(2,1)} collective-permute-done((bf16[2,1024,1536]{2,1,0:T(8,128)(2,1)}, bf16[2,1024,1536]{2,1,0:T(8,128)(2,1)}, u32[]{:S(2)}, u32[]{:S(2)}) %collective-permute-start.15) | collective-permute-done | bytes 6291488 | tf_op jit(solution)/shard_map/ppermute | solution.py:488
  772.9 53.1 %down_part.9 = (bf16[1280,1024]{1,0:T(8,128)(2,1)}, bf16[1280,1024]{1,0:T(8,128)(2,1)}, bf16[1280,1024]{1,0:T(8,128)(2,1)}, bf16[1280,1024]{1,0:T(8,128)(2,1)}) custom-call(s32[6]{0:T(128)} %pad_add_fusion.3.meta_ref, bf16[5120,5632]{1,0:T(8,128)(2,1)} %wide_part.11.refs_0_, bf16[2,5632,1024]{2,1,0:T(8,128)(2,1)} %refs_1_.3), custom_call_target="tpu_custom_call" | custom-call | flops 59055800320 | bytes 57671680 | tf_op jit(solution)/shard_map/down_part/pallas_call | solution.py:299
  826.0 20.0 %collective-permute-start.18 = (bf16[1280,1024]{1,0:T(8,128)(2,1)}, bf16[1280,1024]{1,0:T(8,128)(2,1)}, u32[]{:S(2)}, u32[]{:S(2)}) collective-permute-start(bf16[1280,1024]{1,0:T(8,128)(2,1)} %get-tuple-element.124), channel_id=1, source_target_pairs={{0,3},{1,0},{2,1},{3,2},{4,7},{5,4},{6,5},{7,6}} | collective-permute-start | bytes 7864328 | tf_op jit(solution)/shard_map/ppermute | solution.py:493
  847.7 22.0 %wide_part.12.refs_7_ = bf16[5120,5632]{1,0:T(8,128)(2,1)} custom-call(s32[6]{0:T(128)} %pad_add_fusion.5.meta_ref, bf16[1280,2048]{1,0:T(8,128)(2,1)} %get-tuple-element.99.refs_0_, bf16[1280,2048]{1,0:T(8,128)(2,1)} %collective-permute-done.6.refs_1_, bf16[1280,2048]{1,0:T(8,128)(2,1)} %collective-permute-done.7.refs_2_, ...), custom_call_target="tpu_custom_call" | custom-call | flops 21474836480 | bytes 20971520 | tf_op jit(solution)/shard_map/wide_part/pallas_call | solution.py:183
  869.8 204.9 %collective-permute-done.16.refs_2_ = bf16[5632,512]{1,0:T(8,128)(2,1)} collective-permute-done((bf16[5632,512]{1,0:T(8,128)(2,1)}, bf16[5632,512]{1,0:T(8,128)(2,1)}, u32[]{:S(2)}, u32[]{:S(2)}) %collective-permute-start.16) | collective-permute-done | bytes 5767200 | tf_op jit(solution)/shard_map/ppermute | solution.py:488
  1076.7 79.1 %wide_part.13.refs_7_ = bf16[5120,5632]{1,0:T(8,128)(2,1)} custom-call(s32[6]{0:T(128)} %pad_add_fusion.5.meta_ref, bf16[1280,2048]{1,0:T(8,128)(2,1)} %get-tuple-element.99.refs_0_, bf16[1280,2048]{1,0:T(8,128)(2,1)} %collective-permute-done.6.refs_1_, bf16[1280,2048]{1,0:T(8,128)(2,1)} %collective-permute-done.7.refs_2_, ...), custom_call_target="tpu_custom_call", output_to_operand_aliasing={{}: (8, {})} | custom-call | flops 85899345920 | bytes 20971520 | tf_op jit(solution)/shard_map/wide_part/pallas_call | solution.py:183
  1157.0 59.5 %wide_part.14.refs_7_ = bf16[5120,5632]{1,0:T(8,128)(2,1)} custom-call(s32[6]{0:T(128)} %pad_add_fusion.5.meta_ref, bf16[1280,2048]{1,0:T(8,128)(2,1)} %get-tuple-element.99.refs_0_, bf16[1280,2048]{1,0:T(8,128)(2,1)} %collective-permute-done.6.refs_1_, bf16[1280,2048]{1,0:T(8,128)(2,1)} %collective-permute-done.7.refs_2_, ...), custom_call_target="tpu_custom_call", output_to_operand_aliasing={{}: (8, {})} | custom-call | flops 64424509440 | bytes 20971520 | tf_op jit(solution)/shard_map/wide_part/pallas_call | solution.py:183
  1216.6 118.7 %collective-permute-done.32.refs_2_ = bf16[5632,256]{1,0:T(8,128)(2,1)} collective-permute-done((bf16[5632,256]{1,0:T(8,128)(2,1)}, bf16[5632,256]{1,0:T(8,128)(2,1)}, u32[]{:S(2)}, u32[]{:S(2)}) %collective-permute-start.32) | collective-permute-done | bytes 2883616 | tf_op jit(solution)/shard_map/ppermute | solution.py:488
  1336.8 59.5 %wide_part.15.refs_0_.refs_1_ = bf16[5120,5632]{1,0:T(8,128)(2,1)} custom-call(s32[6]{0:T(128)} %pad_add_fusion.5.meta_ref, bf16[1280,2048]{1,0:T(8,128)(2,1)} %get-tuple-element.99.refs_0_, bf16[1280,2048]{1,0:T(8,128)(2,1)} %collective-permute-done.6.refs_1_, bf16[1280,2048]{1,0:T(8,128)(2,1)} %collective-permute-done.7.refs_2_, ...), custom_call_target="tpu_custom_call", output_to_operand_aliasing={{}: (8, {})} | custom-call | flops 64424509440 | bytes 20971520 | tf_op jit(solution)/shard_map/wide_part/pallas_call | solution.py:183
  1396.3 53.1 %down_part.10 = (bf16[1280,1024]{1,0:T(8,128)(2,1)}, bf16[1280,1024]{1,0:T(8,128)(2,1)}, bf16[1280,1024]{1,0:T(8,128)(2,1)}, bf16[1280,1024]{1,0:T(8,128)(2,1)}) custom-call(s32[6]{0:T(128)} %pad_add_fusion.5.meta_ref, bf16[5120,5632]{1,0:T(8,128)(2,1)} %wide_part.15.refs_0_.refs_1_, bf16[2,5632,1024]{2,1,0:T(8,128)(2,1)} %refs_1_.3), custom_call_target="tpu_custom_call" | custom-call | flops 59055800320 | bytes 57671680 | tf_op jit(solution)/shard_map/down_part/pallas_call | solution.py:299
  1449.4 29.1 %down_part.11 = (bf16[1280,512]{1,0:T(8,128)(2,1)}, bf16[1280,512]{1,0:T(8,128)(2,1)}, bf16[1280,512]{1,0:T(8,128)(2,1)}, bf16[1280,512]{1,0:T(8,128)(2,1)}) custom-call(s32[6]{0:T(128)} %pad_add_fusion.7.meta_ref, bf16[5120,5632]{1,0:T(8,128)(2,1)} %wide_part.11.refs_0_, bf16[5120,5632]{1,0:T(8,128)(2,1)} %wide_part.15.refs_0_.refs_1_, ...), custom_call_target="tpu_custom_call" | custom-call | flops 29527900160 | bytes 57671680 | tf_op jit(solution)/shard_map/down_part/pallas_call | solution.py:299
  1478.5 53.0 %collective-permute-start.19 = (bf16[1280,1024]{1,0:T(8,128)(2,1)}, bf16[1280,1024]{1,0:T(8,128)(2,1)}, u32[]{:S(2)}, u32[]{:S(2)}) collective-permute-start(bf16[1280,1024]{1,0:T(8,128)(2,1)} %get-tuple-element.125), channel_id=1, source_target_pairs={{0,3},{1,0},{2,1},{3,2},{4,7},{5,4},{6,5},{7,6}} | collective-permute-start | bytes 7864328 | tf_op jit(solution)/shard_map/ppermute | solution.py:493
  1531.7 29.9 %down_part.12 = (bf16[1280,512]{1,0:T(8,128)(2,1)}, bf16[1280,512]{1,0:T(8,128)(2,1)}, bf16[1280,512]{1,0:T(8,128)(2,1)}, bf16[1280,512]{1,0:T(8,128)(2,1)}) custom-call(s32[6]{0:T(128)} %pad_add_fusion.6.meta_ref, bf16[5120,5632]{1,0:T(8,128)(2,1)} %wide_part.11.refs_0_, bf16[5120,5632]{1,0:T(8,128)(2,1)} %wide_part.15.refs_0_.refs_1_, ...), custom_call_target="tpu_custom_call" | custom-call | flops 29527900160 | bytes 57671680 | tf_op jit(solution)/shard_map/down_part/pallas_call | solution.py:299
  1561.6 10.8 collective-permute-start.26
  1572.3 16.7 collective-permute-done.19.refs_3_
  1589.1 56.2 %collective-permute-done.21.refs_5_ = bf16[1280,1024]{1,0:T(8,128)(2,1)} collective-permute-done((bf16[1280,1024]{1,0:T(8,128)(2,1)}, bf16[1280,1024]{1,0:T(8,128)(2,1)}, u32[]{:S(2)}, u32[]{:S(2)}) %collective-permute-start.21) | collective-permute-done | bytes 2621472 | tf_op jit(solution)/shard_map/ppermute | solution.py:493
  1647.0 26.3 %mix_cols.5 = (bf16[4096,2048]{1,0:T(8,128)(2,1)}, s32[1]{0:T(128)}) custom-call(s32[1]{0:T(128)} %bitcast.20.col_ref, s32[1024]{0:T(1024)} %mul.93.chunk_ref, s32[4096,2]{1,0:T(8,128)} %copy.40.pos_ref, f32[4096,2]{1,0:T(8,128)} %copy.41.gate_ref, bf16[4096,2048]{1,0:T(8,128)(2,1)} %x_ref.13, bf16[1280,1024]{1,0:T(8,128)(2,1)} %get-tuple-element.114.refs_0_, ...), custom_call_target="tpu_custom_call" | custom-call | flops 20480000000 | bytes 20480000 | tf_op jit(solution)/shard_map/mix_cols/pallas_call | solution.py:389
  1674.5 17.8 down_part.13
  1694.2 7.0 collective-permute-start.29
  1701.4 18.7 down_part.14
  1720.1 6.3 collective-permute-start.33
  1730.6 28.5 %collective-permute-done.29.refs_5_ = bf16[1280,512]{1,0:T(8,128)(2,1)} collective-permute-done((bf16[1280,512]{1,0:T(8,128)(2,1)}, bf16[1280,512]{1,0:T(8,128)(2,1)}, u32[]{:S(2)}, u32[]{:S(2)}) %collective-permute-start.29) | collective-permute-done | bytes 1310752 | tf_op jit(solution)/shard_map/ppermute | solution.py:493
  1760.9 16.9 mix_cols.6
  1779.1 8.2 collective-permute-done.35.refs_4_
  1787.6 17.8 down_part.15
  1805.5 7.8 collective-permute-start.41
  1815.2 12.7 mix_cols.7
  1829.1 18.0 down_part.16
  1847.1 6.5 collective-permute-start.42
  1853.8 18.0 down_part.17
  1879.0 9.6 mix_cols.8
  1893.9 9.6 mix_cols.9
  (188 shorter events, 106.8 us)
Async XLA Ops:
  57.6 233.3 %collective-permute-start = (bf16[1280,2048]{1,0:T(8,128)(2,1)}, bf16[1280,2048]{1,0:T(8,128)(2,1)}, u32[]{:S(2)}, u32[]{:S(2)}) collective-permute-start(bf16[1280,2048]{1,0:T(8,128)(2,1)} %get-tuple-element.95), channel_id=1, source_target_pairs={{0,1},{1,2},{2,3},{3,0},{4,5},{5,6},{6,7},{7,4}} | collective-permute-start | bytes 15728648 | tf_op jit(solution)/shard_map/ppermute | solution.py:493
  57.6 233.3 %collective-permute-start.1 = (bf16[1280,2048]{1,0:T(8,128)(2,1)}, bf16[1280,2048]{1,0:T(8,128)(2,1)}, u32[]{:S(2)}, u32[]{:S(2)}) collective-permute-start(bf16[1280,2048]{1,0:T(8,128)(2,1)} %get-tuple-element.96), channel_id=1, source_target_pairs={{0,2},{1,3},{2,0},{3,1},{4,6},{5,7},{6,4},{7,5}} | collective-permute-start | bytes 15728648 | tf_op jit(solution)/shard_map/ppermute | solution.py:493
  59.6 231.3 %collective-permute-start.2 = (bf16[1280,2048]{1,0:T(8,128)(2,1)}, bf16[1280,2048]{1,0:T(8,128)(2,1)}, u32[]{:S(2)}, u32[]{:S(2)}) collective-permute-start(bf16[1280,2048]{1,0:T(8,128)(2,1)} %get-tuple-element.97), channel_id=1, source_target_pairs={{0,3},{1,0},{2,1},{3,2},{4,7},{5,4},{6,5},{7,6}} | collective-permute-start | bytes 15728648 | tf_op jit(solution)/shard_map/ppermute | solution.py:493
  63.4 104.2 %collective-permute-start.3 = (bf16[1024,512]{1,0:T(8,128)(2,1)}, bf16[1024,512]{1,0:T(8,128)(2,1)}, u32[]{:S(2)}, u32[]{:S(2)}) collective-permute-start(bf16[1024,512]{1,0:T(8,128)(2,1)} %slice_bitcast_fusion.1), channel_id=1, source_target_pairs={{0,4},{4,0},{1,5},{5,1},{2,6},{6,2},{3,7},{7,3}} | collective-permute-start | bytes 3145736 | tf_op jit(solution)/shard_map/ppermute | solution.py:488
  84.0 370.4 %collective-permute-start.9 = (bf16[2,1024,2048]{2,1,0:T(8,128)(2,1)}, bf16[2,1024,2048]{2,1,0:T(8,128)(2,1)}, u32[]{:S(2)}, u32[]{:S(2)}) collective-permute-start(bf16[2,1024,2048]{2,1,0:T(8,128)(2,1)} %pad_maximum_fusion.1), channel_id=1, source_target_pairs={{0,4},{4,0},{1,5},{5,1},{2,6},{6,2},{3,7},{7,3}} | collective-permute-start | bytes 25165832 | tf_op jit(solution)/shard_map/ppermute | solution.py:488
  167.6 122.5 %collective-permute-start.4 = (bf16[1024,512]{1,0:T(8,128)(2,1)}, bf16[1024,512]{1,0:T(8,128)(2,1)}, u32[]{:S(2)}, u32[]{:S(2)}) collective-permute-start(bf16[1024,512]{1,0:T(8,128)(2,1)} %slice_bitcast_fusion), channel_id=1, source_target_pairs={{0,4},{4,0},{1,5},{5,1},{2,6},{6,2},{3,7},{7,3}} | collective-permute-start | bytes 3145736 | tf_op jit(solution)/shard_map/ppermute | solution.py:488
  290.0 163.7 %collective-permute-start.13 = (bf16[2,1024,1536]{2,1,0:T(8,128)(2,1)}, bf16[2,1024,1536]{2,1,0:T(8,128)(2,1)}, u32[]{:S(2)}, u32[]{:S(2)}) collective-permute-start(bf16[2,1024,1536]{2,1,0:T(8,128)(2,1)} %pad_maximum_fusion.5), channel_id=1, source_target_pairs={{0,4},{4,0},{1,5},{5,1},{2,6},{6,2},{3,7},{7,3}} | collective-permute-start | bytes 18874376 | tf_op jit(solution)/shard_map/ppermute | solution.py:488
  312.9 113.1 %collective-permute-start.5 = (s32[4,2]{0,1:T(2,128)S(1)}, s32[4,2]{0,1:T(2,128)S(1)}, u32[]{:S(2)}, u32[]{:S(2)}) collective-permute-start(s32[4,2]{0,1:T(2,128)S(1)} %select_reduce_fusion.4), channel_id=1, source_target_pairs={{0,4},{4,0},{1,5},{5,1},{2,6},{6,2},{3,7},{7,3}} | collective-permute-start | bytes 104 | tf_op jit(solution)/shard_map/ppermute | solution.py:524
  313.0 513.1 %collective-permute-start.6 = (bf16[1280,2048]{1,0:T(8,128)(2,1)}, bf16[1280,2048]{1,0:T(8,128)(2,1)}, u32[]{:S(2)}, u32[]{:S(2)}) collective-permute-start(bf16[1280,2048]{1,0:T(8,128)(2,1)} %get-tuple-element.101), channel_id=1, source_target_pairs={{0,1},{1,2},{2,3},{3,0},{4,5},{5,6},{6,7},{7,4}} | collective-permute-start | bytes 15728648 | tf_op jit(solution)/shard_map/ppermute | solution.py:493
  313.0 533.0 %collective-permute-start.7 = (bf16[1280,2048]{1,0:T(8,128)(2,1)}, bf16[1280,2048]{1,0:T(8,128)(2,1)}, u32[]{:S(2)}, u32[]{:S(2)}) collective-permute-start(bf16[1280,2048]{1,0:T(8,128)(2,1)} %get-tuple-element.103), channel_id=1, source_target_pairs={{0,2},{1,3},{2,0},{3,1},{4,6},{5,7},{6,4},{7,5}} | collective-permute-start | bytes 15728648 | tf_op jit(solution)/shard_map/ppermute | solution.py:493
  426.0 421.6 %collective-permute-start.8 = (bf16[1280,2048]{1,0:T(8,128)(2,1)}, bf16[1280,2048]{1,0:T(8,128)(2,1)}, u32[]{:S(2)}, u32[]{:S(2)}) collective-permute-start(bf16[1280,2048]{1,0:T(8,128)(2,1)} %get-tuple-element.105), channel_id=1, source_target_pairs={{0,3},{1,0},{2,1},{3,2},{4,7},{5,4},{6,5},{7,6}} | collective-permute-start | bytes 15728648 | tf_op jit(solution)/shard_map/ppermute | solution.py:493
  453.7 81.1 %collective-permute-start.14 = (bf16[2,1024,512]{2,1,0:T(8,128)(2,1)}, bf16[2,1024,512]{2,1,0:T(8,128)(2,1)}, u32[]{:S(2)}, u32[]{:S(2)}) collective-permute-start(bf16[2,1024,512]{2,1,0:T(8,128)(2,1)} %pad_maximum_fusion.6), channel_id=1, source_target_pairs={{0,4},{4,0},{1,5},{5,1},{2,6},{6,2},{3,7},{7,3}} | collective-permute-start | bytes 6291464 | tf_op jit(solution)/shard_map/ppermute | solution.py:488
  454.5 182.9 %collective-permute-start.10 = (bf16[2,1024,1536]{2,1,0:T(8,128)(2,1)}, bf16[2,1024,1536]{2,1,0:T(8,128)(2,1)}, u32[]{:S(2)}, u32[]{:S(2)}) collective-permute-start(bf16[2,1024,1536]{2,1,0:T(8,128)(2,1)} %pad_maximum_fusion.3), channel_id=1, source_target_pairs={{0,4},{4,0},{1,5},{5,1},{2,6},{6,2},{3,7},{7,3}} | collective-permute-start | bytes 18874376 | tf_op jit(solution)/shard_map/ppermute | solution.py:488
  534.8 237.3 %collective-permute-start.15 = (bf16[2,1024,1536]{2,1,0:T(8,128)(2,1)}, bf16[2,1024,1536]{2,1,0:T(8,128)(2,1)}, u32[]{:S(2)}, u32[]{:S(2)}) collective-permute-start(bf16[2,1024,1536]{2,1,0:T(8,128)(2,1)} %pad_maximum_fusion.4), channel_id=1, source_target_pairs={{0,4},{4,0},{1,5},{5,1},{2,6},{6,2},{3,7},{7,3}} | collective-permute-start | bytes 18874376 | tf_op jit(solution)/shard_map/ppermute | solution.py:488
  637.3 438.5 %collective-permute-start.11 = (bf16[2,1024,2048]{2,1,0:T(8,128)(2,1)}, bf16[2,1024,2048]{2,1,0:T(8,128)(2,1)}, u32[]{:S(2)}, u32[]{:S(2)}) collective-permute-start(bf16[2,1024,2048]{2,1,0:T(8,128)(2,1)} %pad_maximum_fusion), channel_id=1, source_target_pairs={{0,4},{4,0},{1,5},{5,1},{2,6},{6,2},{3,7},{7,3}} | collective-permute-start | bytes 25165832 | tf_op jit(solution)/shard_map/ppermute | solution.py:488
  772.2 302.5 %collective-permute-start.16 = (bf16[5632,512]{1,0:T(8,128)(2,1)}, bf16[5632,512]{1,0:T(8,128)(2,1)}, u32[]{:S(2)}, u32[]{:S(2)}) collective-permute-start(bf16[5632,512]{1,0:T(8,128)(2,1)} %get-tuple-element.118), channel_id=1, source_target_pairs={{0,4},{4,0},{1,5},{5,1},{2,6},{6,2},{3,7},{7,3}} | collective-permute-start | bytes 17301512 | tf_op jit(solution)/shard_map/ppermute | solution.py:488
  826.0 705.5 %collective-permute-start.18 = (bf16[1280,1024]{1,0:T(8,128)(2,1)}, bf16[1280,1024]{1,0:T(8,128)(2,1)}, u32[]{:S(2)}, u32[]{:S(2)}) collective-permute-start(bf16[1280,1024]{1,0:T(8,128)(2,1)} %get-tuple-element.124), channel_id=1, source_target_pairs={{0,3},{1,0},{2,1},{3,2},{4,7},{5,4},{6,5},{7,6}} | collective-permute-start | bytes 7864328 | tf_op jit(solution)/shard_map/ppermute | solution.py:493
  846.0 715.5 %collective-permute-start.20 = (bf16[1280,1024]{1,0:T(8,128)(2,1)}, bf16[1280,1024]{1,0:T(8,128)(2,1)}, u32[]{:S(2)}, u32[]{:S(2)}) collective-permute-start(bf16[1280,1024]{1,0:T(8,128)(2,1)} %get-tuple-element.126), channel_id=1, source_target_pairs={{0,2},{1,3},{2,0},{3,1},{4,6},{5,7},{6,4},{7,5}} | collective-permute-start | bytes 7864328 | tf_op jit(solution)/shard_map/ppermute | solution.py:493
  847.6 724.8 %collective-permute-start.22 = (bf16[1280,1024]{1,0:T(8,128)(2,1)}, bf16[1280,1024]{1,0:T(8,128)(2,1)}, u32[]{:S(2)}, u32[]{:S(2)}) collective-permute-start(bf16[1280,1024]{1,0:T(8,128)(2,1)} %get-tuple-element.128), channel_id=1, source_target_pairs={{0,1},{1,2},{2,3},{3,0},{4,5},{5,6},{6,7},{7,4}} | collective-permute-start | bytes 7864328 | tf_op jit(solution)/shard_map/ppermute | solution.py:493
  1074.7 81.2 %collective-permute-start.24 = (bf16[5632,256]{1,0:T(8,128)(2,1)}, bf16[5632,256]{1,0:T(8,128)(2,1)}, u32[]{:S(2)}, u32[]{:S(2)}) collective-permute-start(bf16[5632,256]{1,0:T(8,128)(2,1)} %get-tuple-element.131), channel_id=1, source_target_pairs={{0,4},{4,0},{1,5},{5,1},{2,6},{6,2},{3,7},{7,3}} | collective-permute-start | bytes 8650760 | tf_op jit(solution)/shard_map/ppermute | solution.py:488
  1075.8 259.4 %collective-permute-start.12 = (bf16[2,1024,1536]{2,1,0:T(8,128)(2,1)}, bf16[2,1024,1536]{2,1,0:T(8,128)(2,1)}, u32[]{:S(2)}, u32[]{:S(2)}) collective-permute-start(bf16[2,1024,1536]{2,1,0:T(8,128)(2,1)} %pad_maximum_fusion.2), channel_id=1, source_target_pairs={{0,4},{4,0},{1,5},{5,1},{2,6},{6,2},{3,7},{7,3}} | collective-permute-start | bytes 18874376 | tf_op jit(solution)/shard_map/ppermute | solution.py:488
  1155.9 179.4 %collective-permute-start.32 = (bf16[5632,256]{1,0:T(8,128)(2,1)}, bf16[5632,256]{1,0:T(8,128)(2,1)}, u32[]{:S(2)}, u32[]{:S(2)}) collective-permute-start(bf16[5632,256]{1,0:T(8,128)(2,1)} %get-tuple-element.145), channel_id=1, source_target_pairs={{0,4},{4,0},{1,5},{5,1},{2,6},{6,2},{3,7},{7,3}} | collective-permute-start | bytes 8650760 | tf_op jit(solution)/shard_map/ppermute | solution.py:488
  1335.2 196.3 %collective-permute-start.17 = (bf16[5632,512]{1,0:T(8,128)(2,1)}, bf16[5632,512]{1,0:T(8,128)(2,1)}, u32[]{:S(2)}, u32[]{:S(2)}) collective-permute-start(bf16[5632,512]{1,0:T(8,128)(2,1)} %get-tuple-element.121), channel_id=1, source_target_pairs={{0,4},{4,0},{1,5},{5,1},{2,6},{6,2},{3,7},{7,3}} | collective-permute-start | bytes 17301512 | tf_op jit(solution)/shard_map/ppermute | solution.py:488
  1478.5 110.6 %collective-permute-start.19 = (bf16[1280,1024]{1,0:T(8,128)(2,1)}, bf16[1280,1024]{1,0:T(8,128)(2,1)}, u32[]{:S(2)}, u32[]{:S(2)}) collective-permute-start(bf16[1280,1024]{1,0:T(8,128)(2,1)} %get-tuple-element.125), channel_id=1, source_target_pairs={{0,3},{1,0},{2,1},{3,2},{4,7},{5,4},{6,5},{7,6}} | collective-permute-start | bytes 7864328 | tf_op jit(solution)/shard_map/ppermute | solution.py:493
  1531.5 113.7 %collective-permute-start.21 = (bf16[1280,1024]{1,0:T(8,128)(2,1)}, bf16[1280,1024]{1,0:T(8,128)(2,1)}, u32[]{:S(2)}, u32[]{:S(2)}) collective-permute-start(bf16[1280,1024]{1,0:T(8,128)(2,1)} %get-tuple-element.127), channel_id=1, source_target_pairs={{0,2},{1,3},{2,0},{3,1},{4,6},{5,7},{6,4},{7,5}} | collective-permute-start | bytes 7864328 | tf_op jit(solution)/shard_map/ppermute | solution.py:493
  1531.5 115.5 %collective-permute-start.23 = (bf16[1280,1024]{1,0:T(8,128)(2,1)}, bf16[1280,1024]{1,0:T(8,128)(2,1)}, u32[]{:S(2)}, u32[]{:S(2)}) collective-permute-start(bf16[1280,1024]{1,0:T(8,128)(2,1)} %get-tuple-element.129), channel_id=1, source_target_pairs={{0,1},{1,2},{2,3},{3,0},{4,5},{5,6},{6,7},{7,4}} | collective-permute-start | bytes 7864328 | tf_op jit(solution)/shard_map/ppermute | solution.py:493
  1561.6 132.7 %collective-permute-start.26 = (bf16[1280,512]{1,0:T(8,128)(2,1)}, bf16[1280,512]{1,0:T(8,128)(2,1)}, u32[]{:S(2)}, u32[]{:S(2)}) collective-permute-start(bf16[1280,512]{1,0:T(8,128)(2,1)} %get-tuple-element.137), channel_id=1, source_target_pairs={{0,3},{1,0},{2,1},{3,2},{4,7},{5,4},{6,5},{7,6}} | collective-permute-start | bytes 3932168 | tf_op jit(solution)/shard_map/ppermute | solution.py:493
  1572.3 147.7 %collective-permute-start.28 = (bf16[1280,512]{1,0:T(8,128)(2,1)}, bf16[1280,512]{1,0:T(8,128)(2,1)}, u32[]{:S(2)}, u32[]{:S(2)}) collective-permute-start(bf16[1280,512]{1,0:T(8,128)(2,1)} %get-tuple-element.139), channel_id=1, source_target_pairs={{0,2},{1,3},{2,0},{3,1},{4,6},{5,7},{6,4},{7,5}} | collective-permute-start | bytes 3932168 | tf_op jit(solution)/shard_map/ppermute | solution.py:493
  1589.1 131.0 %collective-permute-start.30 = (bf16[1280,512]{1,0:T(8,128)(2,1)}, bf16[1280,512]{1,0:T(8,128)(2,1)}, u32[]{:S(2)}, u32[]{:S(2)}) collective-permute-start(bf16[1280,512]{1,0:T(8,128)(2,1)} %get-tuple-element.141), channel_id=1, source_target_pairs={{0,1},{1,2},{2,3},{3,0},{4,5},{5,6},{6,7},{7,4}} | collective-permute-start | bytes 3932168 | tf_op jit(solution)/shard_map/ppermute | solution.py:493
  1645.2 56.0 %collective-permute-start.25 = (bf16[5632,256]{1,0:T(8,128)(2,1)}, bf16[5632,256]{1,0:T(8,128)(2,1)}, u32[]{:S(2)}, u32[]{:S(2)}) collective-permute-start(bf16[5632,256]{1,0:T(8,128)(2,1)} %get-tuple-element.134), channel_id=1, source_target_pairs={{0,4},{4,0},{1,5},{5,1},{2,6},{6,2},{3,7},{7,3}} | collective-permute-start | bytes 8650760 | tf_op jit(solution)/shard_map/ppermute | solution.py:488
  1692.4 35.4 %collective-permute-start.27 = (bf16[1280,512]{1,0:T(8,128)(2,1)}, bf16[1280,512]{1,0:T(8,128)(2,1)}, u32[]{:S(2)}, u32[]{:S(2)}) collective-permute-start(bf16[1280,512]{1,0:T(8,128)(2,1)} %get-tuple-element.138), channel_id=1, source_target_pairs={{0,3},{1,0},{2,1},{3,2},{4,7},{5,4},{6,5},{7,6}} | collective-permute-start | bytes 3932168 | tf_op jit(solution)/shard_map/ppermute | solution.py:493
  1694.2 65.0 %collective-permute-start.29 = (bf16[1280,512]{1,0:T(8,128)(2,1)}, bf16[1280,512]{1,0:T(8,128)(2,1)}, u32[]{:S(2)}, u32[]{:S(2)}) collective-permute-start(bf16[1280,512]{1,0:T(8,128)(2,1)} %get-tuple-element.140), channel_id=1, source_target_pairs={{0,2},{1,3},{2,0},{3,1},{4,6},{5,7},{6,4},{7,5}} | collective-permute-start | bytes 3932168 | tf_op jit(solution)/shard_map/ppermute | solution.py:493
  1701.2 58.0 %collective-permute-start.31 = (bf16[1280,512]{1,0:T(8,128)(2,1)}, bf16[1280,512]{1,0:T(8,128)(2,1)}, u32[]{:S(2)}, u32[]{:S(2)}) collective-permute-start(bf16[1280,512]{1,0:T(8,128)(2,1)} %get-tuple-element.142), channel_id=1, source_target_pairs={{0,1},{1,2},{2,3},{3,0},{4,5},{5,6},{6,7},{7,4}} | collective-permute-start | bytes 3932168 | tf_op jit(solution)/shard_map/ppermute | solution.py:493
  1720.1 133.6 %collective-permute-start.40 = (bf16[5632,128]{1,0:T(8,128)(2,1)}, bf16[5632,128]{1,0:T(8,128)(2,1)}, u32[]{:S(2)}, u32[]{:S(2)}) collective-permute-start(bf16[5632,128]{1,0:T(8,128)(2,1)} %get-tuple-element.159), channel_id=1, source_target_pairs={{0,4},{4,0},{1,5},{5,1},{2,6},{6,2},{3,7},{7,3}} | collective-permute-start | bytes 4325384 | tf_op jit(solution)/shard_map/ppermute | solution.py:488
  1720.1 58.9 %collective-permute-start.33 = (bf16[1280,256]{1,0:T(8,128)(2,1)}, bf16[1280,256]{1,0:T(8,128)(2,1)S(1)}, u32[]{:S(2)}, u32[]{:S(2)}) collective-permute-start(bf16[1280,256]{1,0:T(8,128)(2,1)} %get-tuple-element.148), channel_id=1, source_target_pairs={{0,3},{1,0},{2,1},{3,2},{4,7},{5,4},{6,5},{7,6}} | collective-permute-start | bytes 1966088 | tf_op jit(solution)/shard_map/ppermute | solution.py:493
  1727.8 59.5 %collective-permute-start.35 = (bf16[1280,256]{1,0:T(8,128)(2,1)}, bf16[1280,256]{1,0:T(8,128)(2,1)}, u32[]{:S(2)}, u32[]{:S(2)}) collective-permute-start(bf16[1280,256]{1,0:T(8,128)(2,1)} %get-tuple-element.150), channel_id=1, source_target_pairs={{0,2},{1,3},{2,0},{3,1},{4,6},{5,7},{6,4},{7,5}} | collective-permute-start | bytes 1966088 | tf_op jit(solution)/shard_map/ppermute | solution.py:493
  1759.2 28.1 %collective-permute-start.37 = (bf16[1280,256]{1,0:T(8,128)(2,1)}, bf16[1280,256]{1,0:T(8,128)(2,1)}, u32[]{:S(2)}, u32[]{:S(2)}) collective-permute-start(bf16[1280,256]{1,0:T(8,128)(2,1)} %get-tuple-element.152), channel_id=1, source_target_pairs={{0,1},{1,2},{2,3},{3,0},{4,5},{5,6},{6,7},{7,4}} | collective-permute-start | bytes 1966088 | tf_op jit(solution)/shard_map/ppermute | solution.py:493
  1759.2 46.3 %collective-permute-start.34 = (bf16[1280,256]{1,0:T(8,128)(2,1)}, bf16[1280,256]{1,0:T(8,128)(2,1)}, u32[]{:S(2)}, u32[]{:S(2)}) collective-permute-start(bf16[1280,256]{1,0:T(8,128)(2,1)} %get-tuple-element.149), channel_id=1, source_target_pairs={{0,3},{1,0},{2,1},{3,2},{4,7},{5,4},{6,5},{7,6}} | collective-permute-start | bytes 1966088 | tf_op jit(solution)/shard_map/ppermute | solution.py:493
  1779.1 36.1 %collective-permute-start.36 = (bf16[1280,256]{1,0:T(8,128)(2,1)}, bf16[1280,256]{1,0:T(8,128)(2,1)}, u32[]{:S(2)}, u32[]{:S(2)}) collective-permute-start(bf16[1280,256]{1,0:T(8,128)(2,1)} %get-tuple-element.151), channel_id=1, source_target_pairs={{0,2},{1,3},{2,0},{3,1},{4,6},{5,7},{6,4},{7,5}} | collective-permute-start | bytes 1966088 | tf_op jit(solution)/shard_map/ppermute | solution.py:493
  1787.3 27.9 %collective-permute-start.38 = (bf16[1280,256]{1,0:T(8,128)(2,1)}, bf16[1280,256]{1,0:T(8,128)(2,1)}, u32[]{:S(2)}, u32[]{:S(2)}) collective-permute-start(bf16[1280,256]{1,0:T(8,128)(2,1)} %get-tuple-element.153), channel_id=1, source_target_pairs={{0,1},{1,2},{2,3},{3,0},{4,5},{5,6},{6,7},{7,4}} | collective-permute-start | bytes 1966088 | tf_op jit(solution)/shard_map/ppermute | solution.py:493
  1787.3 41.8 %collective-permute-start.39 = (bf16[5632,128]{1,0:T(8,128)(2,1)}, bf16[5632,128]{1,0:T(8,128)(2,1)}, u32[]{:S(2)}, u32[]{:S(2)}) collective-permute-start(bf16[5632,128]{1,0:T(8,128)(2,1)} %get-tuple-element.156), channel_id=1, source_target_pairs={{0,4},{4,0},{1,5},{5,1},{2,6},{6,2},{3,7},{7,3}} | collective-permute-start | bytes 4325384 | tf_op jit(solution)/shard_map/ppermute | solution.py:488
  1805.5 48.1 %collective-permute-start.41 = (bf16[1280,256]{1,0:T(8,128)(2,1)}, bf16[1280,256]{1,0:T(8,128)(2,1)S(1)}, u32[]{:S(2)}, u32[]{:S(2)}) collective-permute-start(bf16[1280,256]{1,0:T(8,128)(2,1)} %get-tuple-element.162), channel_id=1, source_target_pairs={{0,3},{1,0},{2,1},{3,2},{4,7},{5,4},{6,5},{7,6}} | collective-permute-start | bytes 1966088 | tf_op jit(solution)/shard_map/ppermute | solution.py:493
  1815.2 56.7 %collective-permute-start.43 = (bf16[1280,256]{1,0:T(8,128)(2,1)}, bf16[1280,256]{1,0:T(8,128)(2,1)}, u32[]{:S(2)}, u32[]{:S(2)}) collective-permute-start(bf16[1280,256]{1,0:T(8,128)(2,1)} %get-tuple-element.164), channel_id=1, source_target_pairs={{0,2},{1,3},{2,0},{3,1},{4,6},{5,7},{6,4},{7,5}} | collective-permute-start | bytes 1966088 | tf_op jit(solution)/shard_map/ppermute | solution.py:493
  1815.2 63.0 %collective-permute-start.45 = (bf16[1280,256]{1,0:T(8,128)(2,1)}, bf16[1280,256]{1,0:T(8,128)(2,1)}, u32[]{:S(2)}, u32[]{:S(2)}) collective-permute-start(bf16[1280,256]{1,0:T(8,128)(2,1)} %get-tuple-element.166), channel_id=1, source_target_pairs={{0,1},{1,2},{2,3},{3,0},{4,5},{5,6},{6,7},{7,4}} | collective-permute-start | bytes 1966088 | tf_op jit(solution)/shard_map/ppermute | solution.py:493
  1847.1 31.1 %collective-permute-start.42 = (bf16[1280,128]{1,0:T(8,128)(2,1)}, bf16[1280,128]{1,0:T(8,128)(2,1)S(1)}, u32[]{:S(2)}, u32[]{:S(2)}) collective-permute-start(bf16[1280,128]{1,0:T(8,128)(2,1)} %get-tuple-element.163), channel_id=1, source_target_pairs={{0,3},{1,0},{2,1},{3,2},{4,7},{5,4},{6,5},{7,6}} | collective-permute-start | bytes 983048 | tf_op jit(solution)/shard_map/ppermute | solution.py:493
  1853.6 24.7 %collective-permute-start.44 = (bf16[1280,128]{1,0:T(8,128)(2,1)}, bf16[1280,128]{1,0:T(8,128)(2,1)}, u32[]{:S(2)}, u32[]{:S(2)}) collective-permute-start(bf16[1280,128]{1,0:T(8,128)(2,1)} %get-tuple-element.165), channel_id=1, source_target_pairs={{0,2},{1,3},{2,0},{3,1},{4,6},{5,7},{6,4},{7,5}} | collective-permute-start | bytes 983048 | tf_op jit(solution)/shard_map/ppermute | solution.py:493
  1853.7 24.7 %collective-permute-start.46 = (bf16[1280,128]{1,0:T(8,128)(2,1)}, bf16[1280,128]{1,0:T(8,128)(2,1)}, u32[]{:S(2)}, u32[]{:S(2)}) collective-permute-start(bf16[1280,128]{1,0:T(8,128)(2,1)} %get-tuple-element.167), channel_id=1, source_target_pairs={{0,1},{1,2},{2,3},{3,0},{4,5},{5,6},{6,7},{7,4}} | collective-permute-start | bytes 983048 | tf_op jit(solution)/shard_map/ppermute | solution.py:493
  1871.9 17.3 collective-permute-start.47
  (17 other events, 238.0 us)
where the time goes:
time: 1910 us; the launch traced here: 1900 us
  Pallas kernels  857 us (45%)
  waiting for transfers between devices  762 us (40%)
  starting transfers between devices  155 us (8%)
  local copies, waits for them, and re-layouts  70.1 us (4%)
  other arithmetic  48.3 us (3%)
    ppermute x16, waiting for transfers between devices, cross(): far.append(lax.ppermute(piece, 'data', swap))  542 us
    pallas_call x8, Pallas kernels, wide_part(): pl.pallas_call(functools.partial(wide_body, n_group, len(far), local, lo_...  440 us
    pallas_call x9, Pallas kernels, down_part(): pl.pallas_call(functools.partial(down_body, segs, local, deep, pair_size,...  256 us
    ppermute x33, starting transfers between devices, exchange(): lax.ppermute(blocks[d], 'expert', [(s, (s + step * d) % n_group) for s in...  141 us
    ppermute x33, waiting for transfers between devices, exchange(): lax.ppermute(blocks[d], 'expert', [(s, (s + step * d) % n_group) for s in...  117 us
    ppermute x1, waiting for transfers between devices, whole_step(): totals += lax.ppermute(totals, 'data', swap)  103 us
    pallas_call x2, Pallas kernels, pack_rows(): pl.pallas_call(functools.partial(pack_body, n_local, local, n_blk, n_grou...  85.7 us
    pallas_call x5, Pallas kernels, mix_cols(): pl.pallas_call(functools.partial(mix_body, n_exp, tok_rows // MIX_TILE, t...  75 us
  transfers between devices with their start and end apart: 50, of which 13 were waited for; matrix products, arithmetic and copies ran while one was open for 6% of the time, Pallas kernels for 42%

commit v1 on v0

--- a/solution.py
+++ b/solution.py
@@ -315,13 +315,13 @@
     )(meta, *hidden, weight)
 
 
-def mix_body(n_exp, n_tile, subs, widths, unroll, col_ref, chunk_ref, pos_ref, gate_ref, x_ref, *refs):
+def mix_body(n_exp, n_tile, subs, widths, unroll, col_ref, chunk_ref, pair_ref, x_ref, *refs):
     n_set = len(widths)
     back_refs = refs[: n_set * n_exp]
-    y_ref, mark_ref, pos_buf, gate_buf = refs[-6 - 4 * n_set : -2 - 4 * n_set]
+    y_ref, mark_ref, pair_buf = refs[-5 - 4 * n_set : -2 - 4 * n_set]
     bufs, sems, y_sems = refs[-2 - 4 * n_set : -2], refs[-2], refs[-1]
     sets = []
-    copies = [pltpu.make_async_copy(pos_ref, pos_buf, sems.at[0]), pltpu.make_async_copy(gate_ref, gate_buf, sems.at[1])]
+    copies = [pltpu.make_async_copy(pair_ref, pair_buf, sems.at[0])]
     for g, width in enumerate(widths):
         back_buf, near_buf, x_buf, y_buf = bufs[4 * g : 4 * g + 4]
         cols = pl.ds(pl.multiple_of(col_ref[g], 128), width)
@@ -347,13 +347,13 @@
             i = block * unroll + k
             tokens = pl.ds(pl.multiple_of(i * MIX_TILE, MIX_TILE), MIX_TILE)
             seat = lax.broadcasted_iota(I32, (MIX_TILE, REACH), 1)
-            pick = jnp.concatenate([(seat == pos_buf[tokens, j : j + 1]).astype(F32).astype(BF16) for j in range(2)], axis=0)
+            pick = jnp.concatenate([(seat == pair_buf[tokens, j : j + 1].astype(I32)).astype(F32).astype(BF16) for j in range(2)], axis=0)
             for back_buf, near_buf, x_buf, y_buf, _ in sets:
                 for c in range(REACH // ALIGN):
                     chunk = pl.multiple_of(chunk_ref[i * (REACH // ALIGN) + c], ALIGN)
                     near_buf[k, c * ALIGN : (c + 1) * ALIGN, :] = back_buf[pl.ds(chunk, ALIGN), :]
                 found = jnp.dot(pick, near_buf[k], preferred_element_type=F32)
-                mixed = gate_buf[tokens, 0:1] * found[:MIX_TILE] + gate_buf[tokens, 1:2] * found[MIX_TILE:]
+                mixed = pair_buf[tokens, 2:3] * found[:MIX_TILE] + pair_buf[tokens, 3:4] * found[MIX_TILE:]
                 y_buf[tokens, :] = (x_buf[tokens, :].astype(F32) + mixed).astype(BF16)
         for g in range(n_set):
             out(g, block).start()
@@ -366,19 +366,19 @@
     mark_ref[0] = 0
 
 
-def mix_cols(col, y_loc, x_loc, pos, gate_loc, chunks, widths, back):
+def mix_cols(col, y_loc, x_loc, pairs, chunks, widths, back):
     tok_rows, d_model = x_loc.shape
     n_exp = len(back) // len(widths)
     capacity = back[0][0].shape[0]
-    unroll = 4 if sum(widths) < 256 else 2
-    args = [col, chunks, pos, gate_loc, x_loc, *[array for array, _ in back]]
-    specs = [smem(), smem()] + [any_spec()] * (3 + len(back))
+    unroll = 8 if sum(widths) < 256 else 4 if sum(widths) < 512 else 2
+    args = [col, chunks, pairs, x_loc, *[array for array, _ in back]]
+    specs = [smem(), smem()] + [any_spec()] * (2 + len(back))
     alias = {}
     if y_loc is not None:
         alias = {len(args): 0}
         args.append(y_loc)
         specs.append(any_spec())
-    bufs = [pltpu.VMEM(pos.shape, I32), pltpu.VMEM(gate_loc.shape, F32)]
+    bufs = [pltpu.VMEM(pairs.shape, F32)]
     for width in widths:
         bufs += [
             pltpu.VMEM((n_exp * capacity, width), BF16),
@@ -392,7 +392,7 @@
         out_specs=[any_spec(), smem()],
         scratch_shapes=bufs
         + [
-            pltpu.SemaphoreType.DMA((2 + (n_exp + 1) * len(widths),)),
+            pltpu.SemaphoreType.DMA((1 + (n_exp + 1) * len(widths),)),
             pltpu.SemaphoreType.DMA((len(widths), tok_rows // MIX_TILE // unroll)),
         ],
         out_shape=[jax.ShapeDtypeStruct((tok_rows, d_model), BF16), jax.ShapeDtypeStruct((1,), I32)],
@@ -455,6 +455,7 @@
         at = slot_te + jnp.repeat((lead - start) * ALIGN, MIX_TILE, axis=1)
         at = jnp.where(slot_te < 0, -1, at)
         pos = jnp.stack([jnp.sum(jnp.where(ids[j][None, :] == experts, at, 0), axis=0) for j in range(top_k)], axis=1)
+        pairs = jnp.concatenate([pos.astype(F32), gate_loc], axis=1)
         seat = jnp.arange(reach, dtype=I32)[None, None, :]
         taken = (seat >= lead[:, :, None]) & (seat < (lead + size)[:, :, None])
 
@@ -496,7 +497,7 @@
         def mix(y_loc, chunks, *sets):
             col = jnp.stack([col for col, _, _ in sets]).astype(I32)
             back = [(pair[l][0][d], pair[l][1]) for _, _, pair in sets for d in range(n_group) for l in locals_]
-            out = in_turn(mix_cols, col, y_loc, x_loc, pos, gate_loc, chunks, tuple(width for _, width, _ in sets), back)
+            out = in_turn(mix_cols, col, y_loc, x_loc, pairs, chunks, tuple(width for _, width, _ in sets), back)
             done[-1] = out[1][0]
             return out[0]
 

time: 1910 us -> 1900 us (level)
  transfers between devices with their start and end apart: 50 -> 50, of which waited for: 13 -> 13; matrix products, arithmetic and copies ran while one was open for 6% -> 5% of each run, Pallas kernels for 42% -> 42%
where the time goes in v1:
time: 1900 us
  Pallas kernels  851 us (45%)
  waiting for transfers between devices  766 us (40%)
  starting transfers between devices  155 us (8%)
  local copies, waits for them, and re-layouts  68.2 us (4%)
  other arithmetic  48.5 us (3%)
    ppermute x16, waiting for transfers between devices, cross(): far.append(lax.ppermute(piece, 'data', swap))  544 us
    pallas_call x8, Pallas kernels, wide_part(): pl.pallas_call(functools.partial(wide_body, n_group, len(far), local, lo_...  440 us
    pallas_call x9, Pallas kernels, down_part(): pl.pallas_call(functools.partial(down_body, segs, local, deep, pair_size,...  256 us
    ppermute x33, starting transfers between devices, exchange(): lax.ppermute(blocks[d], 'expert', [(s, (s + step * d) % n_group) for s in...  140 us
    ppermute x33, waiting for transfers between devices, exchange(): lax.ppermute(blocks[d], 'expert', [(s, (s + step * d) % n_group) for s in...  119 us
    ppermute x1, waiting for transfers between devices, whole_step(): totals += lax.ppermute(totals, 'data', swap)  103 us
    pallas_call x2, Pallas kernels, pack_rows(): pl.pallas_call(functools.partial(pack_body, n_local, local, n_blk, n_grou...  85.7 us
    pallas_call x5, Pallas kernels, mix_cols(): pl.pallas_call(functools.partial(mix_body, n_exp, tok_rows // MIX_TILE, t...  68.8 us
  transfers between devices with their start and end apart: 50, of which 13 were waited for; matrix products, arithmetic and copies ran while one was open for 5% of the time, Pallas kernels for 42%

profile of v1, /device:TPU:0, one launch (start us, length us, event | category | flops | bytes accessed | tf_op | source)
XLA Modules:
  0.0 1899.9 jit_solution(16450894985091870470)
XLA Ops:
  6.4 6.7 all-reduce
  17.1 40.5 %pack_rows.2 = (bf16[1280,2048]{1,0:T(8,128)(2,1)}, bf16[1280,2048]{1,0:T(8,128)(2,1)}, bf16[1280,2048]{1,0:T(8,128)(2,1)}, bf16[1280,2048]{1,0:T(8,128)(2,1)}) custom-call(s32[136]{0:T(256)} %reshape.418.first_ref, s32[8,4096]{1,0:T(8,128)} %get-tuple-element.206.slot_ref, bf16[4096,2048]{1,0:T(8,128)(2,1)} %x_ref.13), custom_call_target="tpu_custom_call" | custom-call | flops 20000000000 | bytes 60000000 | tf_op jit(solution)/shard_map/pack_rows/pallas_call | solution.py:83
  66.2 11.4 fusion.28
  77.6 6.3 pad_maximum_fusion.1
  85.4 17.8 fusion.26
  116.1 45.2 %pack_rows.3 = (bf16[1280,2048]{1,0:T(8,128)(2,1)}, bf16[1280,2048]{1,0:T(8,128)(2,1)}, bf16[1280,2048]{1,0:T(8,128)(2,1)}, bf16[1280,2048]{1,0:T(8,128)(2,1)}) custom-call(s32[136]{0:T(256)} %reshape.418.first_ref, s32[8,4096]{1,0:T(8,128)} %get-tuple-element.206.slot_ref, bf16[4096,2048]{1,0:T(8,128)(2,1)} %x_ref.13), custom_call_target="tpu_custom_call" | custom-call | flops 20000000000 | bytes 60000000 | tf_op jit(solution)/shard_map/pack_rows/pallas_call | solution.py:83
  186.8 103.1 %collective-permute-done.4.refs_7_ = bf16[1024,512]{1,0:T(8,128)(2,1)} collective-permute-done((bf16[1024,512]{1,0:T(8,128)(2,1)}, bf16[1024,512]{1,0:T(8,128)(2,1)}, u32[]{:S(2)}, u32[]{:S(2)}) %collective-permute-start.4) | collective-permute-done | bytes 1048608 | tf_op jit(solution)/shard_map/ppermute | solution.py:489
  290.8 22.0 %wide_part.8.refs_7_ = bf16[5120,5632]{1,0:T(8,128)(2,1)} custom-call(s32[6]{0:T(128)} %pad_add_fusion.2.meta_ref, bf16[1280,2048]{1,0:T(8,128)(2,1)} %get-tuple-element.91.refs_0_, bf16[1280,2048]{1,0:T(8,128)(2,1)} %collective-permute-done.refs_1_, bf16[1280,2048]{1,0:T(8,128)(2,1)} %collective-permute-done.1.refs_2_, ...), custom_call_target="tpu_custom_call" | custom-call | flops 21474836480 | bytes 20971520 | tf_op jit(solution)/shard_map/wide_part/pallas_call | solution.py:183
  312.9 10.2 collective-permute-start.7
  323.2 102.8 %collective-permute-done.5 = s32[4,2]{0,1:T(2,128)S(1)} collective-permute-done((s32[4,2]{0,1:T(2,128)S(1)}, s32[4,2]{0,1:T(2,128)S(1)}, u32[]{:S(2)}, u32[]{:S(2)}) %collective-permute-start.5) | collective-permute-done | bytes 64 | tf_op jit(solution)/shard_map/ppermute | solution.py:525
  437.2 7.0 dynamic-slice_bitcast_fusion.2
  444.3 9.3 dynamic-slice_bitcast_fusion
  455.6 79.1 %wide_part.9.refs_7_ = bf16[5120,5632]{1,0:T(8,128)(2,1)} custom-call(s32[6]{0:T(128)} %pad_add_fusion.2.meta_ref, bf16[1280,2048]{1,0:T(8,128)(2,1)} %get-tuple-element.91.refs_0_, bf16[1280,2048]{1,0:T(8,128)(2,1)} %collective-permute-done.refs_1_, bf16[1280,2048]{1,0:T(8,128)(2,1)} %collective-permute-done.1.refs_2_, ...), custom_call_target="tpu_custom_call", output_to_operand_aliasing={{}: (8, {})} | custom-call | flops 85899345920 | bytes 20971520 | tf_op jit(solution)/shard_map/wide_part/pallas_call | solution.py:183
  534.8 59.5 %wide_part.10.refs_7_ = bf16[5120,5632]{1,0:T(8,128)(2,1)} custom-call(s32[6]{0:T(128)} %pad_add_fusion.2.meta_ref, bf16[1280,2048]{1,0:T(8,128)(2,1)} %get-tuple-element.91.refs_0_, bf16[1280,2048]{1,0:T(8,128)(2,1)} %collective-permute-done.refs_1_, bf16[1280,2048]{1,0:T(8,128)(2,1)} %collective-permute-done.1.refs_2_, ...), custom_call_target="tpu_custom_call", output_to_operand_aliasing={{}: (8, {})} | custom-call | flops 64424509440 | bytes 20971520 | tf_op jit(solution)/shard_map/wide_part/pallas_call | solution.py:183
  594.3 42.9 %collective-permute-done.10.refs_6_ = bf16[2,1024,1536]{2,1,0:T(8,128)(2,1)} collective-permute-done((bf16[2,1024,1536]{2,1,0:T(8,128)(2,1)}, bf16[2,1024,1536]{2,1,0:T(8,128)(2,1)}, u32[]{:S(2)}, u32[]{:S(2)}) %collective-permute-start.10) | collective-permute-done | bytes 6291488 | tf_op jit(solution)/shard_map/ppermute | solution.py:489
  638.0 59.6 %wide_part.11.refs_0_ = bf16[5120,5632]{1,0:T(8,128)(2,1)} custom-call(s32[6]{0:T(128)} %pad_add_fusion.2.meta_ref, bf16[1280,2048]{1,0:T(8,128)(2,1)} %get-tuple-element.91.refs_0_, bf16[1280,2048]{1,0:T(8,128)(2,1)} %collective-permute-done.refs_1_, bf16[1280,2048]{1,0:T(8,128)(2,1)} %collective-permute-done.1.refs_2_, ...), custom_call_target="tpu_custom_call", output_to_operand_aliasing={{}: (8, {})} | custom-call | flops 64424509440 | bytes 20971520 | tf_op jit(solution)/shard_map/wide_part/pallas_call | solution.py:183
  697.6 74.4 %collective-permute-done.15.refs_6_ = bf16[2,1024,1536]{2,1,0:T(8,128)(2,1)} collective-permute-done((bf16[2,1024,1536]{2,1,0:T(8,128)(2,1)}, bf16[2,1024,1536]{2,1,0:T(8,128)(2,1)}, u32[]{:S(2)}, u32[]{:S(2)}) %collective-permute-start.15) | collective-permute-done | bytes 6291488 | tf_op jit(solution)/shard_map/ppermute | solution.py:489
  772.9 53.1 %down_part.9 = (bf16[1280,1024]{1,0:T(8,128)(2,1)}, bf16[1280,1024]{1,0:T(8,128)(2,1)}, bf16[1280,1024]{1,0:T(8,128)(2,1)}, bf16[1280,1024]{1,0:T(8,128)(2,1)}) custom-call(s32[6]{0:T(128)} %pad_add_fusion.2.meta_ref, bf16[5120,5632]{1,0:T(8,128)(2,1)} %wide_part.11.refs_0_, bf16[2,5632,1024]{2,1,0:T(8,128)(2,1)} %refs_1_.3), custom_call_target="tpu_custom_call" | custom-call | flops 59055800320 | bytes 57671680 | tf_op jit(solution)/shard_map/down_part/pallas_call | solution.py:299
  825.9 20.0 %collective-permute-start.18 = (bf16[1280,1024]{1,0:T(8,128)(2,1)}, bf16[1280,1024]{1,0:T(8,128)(2,1)}, u32[]{:S(2)}, u32[]{:S(2)}) collective-permute-start(bf16[1280,1024]{1,0:T(8,128)(2,1)} %get-tuple-element.124), channel_id=1, source_target_pairs={{0,3},{1,0},{2,1},{3,2},{4,7},{5,4},{6,5},{7,6}} | collective-permute-start | bytes 7864328 | tf_op jit(solution)/shard_map/ppermute | solution.py:494
  847.7 22.0 %wide_part.12.refs_7_ = bf16[5120,5632]{1,0:T(8,128)(2,1)} custom-call(s32[6]{0:T(128)} %pad_add_fusion.4.meta_ref, bf16[1280,2048]{1,0:T(8,128)(2,1)} %get-tuple-element.99.refs_0_, bf16[1280,2048]{1,0:T(8,128)(2,1)} %collective-permute-done.6.refs_1_, bf16[1280,2048]{1,0:T(8,128)(2,1)} %collective-permute-done.7.refs_2_, ...), custom_call_target="tpu_custom_call" | custom-call | flops 21474836480 | bytes 20971520 | tf_op jit(solution)/shard_map/wide_part/pallas_call | solution.py:183
  869.7 204.9 %collective-permute-done.16.refs_2_ = bf16[5632,512]{1,0:T(8,128)(2,1)} collective-permute-done((bf16[5632,512]{1,0:T(8,128)(2,1)}, bf16[5632,512]{1,0:T(8,128)(2,1)}, u32[]{:S(2)}, u32[]{:S(2)}) %collective-permute-start.16) | collective-permute-done | bytes 5767200 | tf_op jit(solution)/shard_map/ppermute | solution.py:489
  1076.6 79.1 %wide_part.13.refs_7_ = bf16[5120,5632]{1,0:T(8,128)(2,1)} custom-call(s32[6]{0:T(128)} %pad_add_fusion.4.meta_ref, bf16[1280,2048]{1,0:T(8,128)(2,1)} %get-tuple-element.99.refs_0_, bf16[1280,2048]{1,0:T(8,128)(2,1)} %collective-permute-done.6.refs_1_, bf16[1280,2048]{1,0:T(8,128)(2,1)} %collective-permute-done.7.refs_2_, ...), custom_call_target="tpu_custom_call", output_to_operand_aliasing={{}: (8, {})} | custom-call | flops 85899345920 | bytes 20971520 | tf_op jit(solution)/shard_map/wide_part/pallas_call | solution.py:183
  1157.0 59.5 %wide_part.14.refs_7_ = bf16[5120,5632]{1,0:T(8,128)(2,1)} custom-call(s32[6]{0:T(128)} %pad_add_fusion.4.meta_ref, bf16[1280,2048]{1,0:T(8,128)(2,1)} %get-tuple-element.99.refs_0_, bf16[1280,2048]{1,0:T(8,128)(2,1)} %collective-permute-done.6.refs_1_, bf16[1280,2048]{1,0:T(8,128)(2,1)} %collective-permute-done.7.refs_2_, ...), custom_call_target="tpu_custom_call", output_to_operand_aliasing={{}: (8, {})} | custom-call | flops 64424509440 | bytes 20971520 | tf_op jit(solution)/shard_map/wide_part/pallas_call | solution.py:183
  1216.5 118.6 %collective-permute-done.32.refs_2_ = bf16[5632,256]{1,0:T(8,128)(2,1)} collective-permute-done((bf16[5632,256]{1,0:T(8,128)(2,1)}, bf16[5632,256]{1,0:T(8,128)(2,1)}, u32[]{:S(2)}, u32[]{:S(2)}) %collective-permute-start.32) | collective-permute-done | bytes 2883616 | tf_op jit(solution)/shard_map/ppermute | solution.py:489
  1336.7 59.5 %wide_part.15.refs_0_.refs_1_ = bf16[5120,5632]{1,0:T(8,128)(2,1)} custom-call(s32[6]{0:T(128)} %pad_add_fusion.4.meta_ref, bf16[1280,2048]{1,0:T(8,128)(2,1)} %get-tuple-element.99.refs_0_, bf16[1280,2048]{1,0:T(8,128)(2,1)} %collective-permute-done.6.refs_1_, bf16[1280,2048]{1,0:T(8,128)(2,1)} %collective-permute-done.7.refs_2_, ...), custom_call_target="tpu_custom_call", output_to_operand_aliasing={{}: (8, {})} | custom-call | flops 64424509440 | bytes 20971520 | tf_op jit(solution)/shard_map/wide_part/pallas_call | solution.py:183
  1396.3 53.1 %down_part.10 = (bf16[1280,1024]{1,0:T(8,128)(2,1)}, bf16[1280,1024]{1,0:T(8,128)(2,1)}, bf16[1280,1024]{1,0:T(8,128)(2,1)}, bf16[1280,1024]{1,0:T(8,128)(2,1)}) custom-call(s32[6]{0:T(128)} %pad_add_fusion.4.meta_ref, bf16[5120,5632]{1,0:T(8,128)(2,1)} %wide_part.15.refs_0_.refs_1_, bf16[2,5632,1024]{2,1,0:T(8,128)(2,1)} %refs_1_.3), custom_call_target="tpu_custom_call" | custom-call | flops 59055800320 | bytes 57671680 | tf_op jit(solution)/shard_map/down_part/pallas_call | solution.py:299
  1449.3 29.1 %down_part.11 = (bf16[1280,512]{1,0:T(8,128)(2,1)}, bf16[1280,512]{1,0:T(8,128)(2,1)}, bf16[1280,512]{1,0:T(8,128)(2,1)}, bf16[1280,512]{1,0:T(8,128)(2,1)}) custom-call(s32[6]{0:T(128)} %pad_add_fusion.6.meta_ref, bf16[5120,5632]{1,0:T(8,128)(2,1)} %wide_part.11.refs_0_, bf16[5120,5632]{1,0:T(8,128)(2,1)} %wide_part.15.refs_0_.refs_1_, ...), custom_call_target="tpu_custom_call" | custom-call | flops 29527900160 | bytes 57671680 | tf_op jit(solution)/shard_map/down_part/pallas_call | solution.py:299
  1478.4 53.0 %collective-permute-start.19 = (bf16[1280,1024]{1,0:T(8,128)(2,1)}, bf16[1280,1024]{1,0:T(8,128)(2,1)}, u32[]{:S(2)}, u32[]{:S(2)}) collective-permute-start(bf16[1280,1024]{1,0:T(8,128)(2,1)} %get-tuple-element.125), channel_id=1, source_target_pairs={{0,3},{1,0},{2,1},{3,2},{4,7},{5,4},{6,5},{7,6}} | collective-permute-start | bytes 7864328 | tf_op jit(solution)/shard_map/ppermute | solution.py:494
  1531.6 29.9 %down_part.12 = (bf16[1280,512]{1,0:T(8,128)(2,1)}, bf16[1280,512]{1,0:T(8,128)(2,1)}, bf16[1280,512]{1,0:T(8,128)(2,1)}, bf16[1280,512]{1,0:T(8,128)(2,1)}) custom-call(s32[6]{0:T(128)} %pad_add_fusion.5.meta_ref, bf16[5120,5632]{1,0:T(8,128)(2,1)} %wide_part.11.refs_0_, bf16[5120,5632]{1,0:T(8,128)(2,1)} %wide_part.15.refs_0_.refs_1_, ...), custom_call_target="tpu_custom_call" | custom-call | flops 29527900160 | bytes 57671680 | tf_op jit(solution)/shard_map/down_part/pallas_call | solution.py:299
  1561.5 10.8 collective-permute-start.26
  1572.3 16.7 collective-permute-done.19.refs_3_
  1589.0 56.2 %collective-permute-done.21.refs_5_ = bf16[1280,1024]{1,0:T(8,128)(2,1)} collective-permute-done((bf16[1280,1024]{1,0:T(8,128)(2,1)}, bf16[1280,1024]{1,0:T(8,128)(2,1)}, u32[]{:S(2)}, u32[]{:S(2)}) %collective-permute-start.21) | collective-permute-done | bytes 2621472 | tf_op jit(solution)/shard_map/ppermute | solution.py:494
  1646.9 25.6 %mix_cols.5 = (bf16[4096,2048]{1,0:T(8,128)(2,1)}, s32[1]{0:T(128)}) custom-call(s32[1]{0:T(128)} %bitcast.20.col_ref, s32[1024]{0:T(1024)} %mul.93.chunk_ref, f32[4096,4]{1,0:T(8,128)} %copy.27.pair_ref, bf16[4096,2048]{1,0:T(8,128)(2,1)} %x_ref.13, bf16[1280,1024]{1,0:T(8,128)(2,1)} %get-tuple-element.114.refs_0_, ...), custom_call_target="tpu_custom_call" | custom-call | flops 20480000000 | bytes 20480000 | tf_op jit(solution)/shard_map/mix_cols/pallas_call | solution.py:389
  1673.8 17.8 down_part.13
  1693.5 7.1 collective-permute-start.29
  1700.8 18.7 down_part.14
  1719.5 6.3 collective-permute-start.33
  1730.0 28.5 %collective-permute-done.29.refs_5_ = bf16[1280,512]{1,0:T(8,128)(2,1)} collective-permute-done((bf16[1280,512]{1,0:T(8,128)(2,1)}, bf16[1280,512]{1,0:T(8,128)(2,1)}, u32[]{:S(2)}, u32[]{:S(2)}) %collective-permute-start.29) | collective-permute-done | bytes 1310752 | tf_op jit(solution)/shard_map/ppermute | solution.py:494
  1760.3 16.4 mix_cols.6
  1778.3 8.3 collective-permute-done.35.refs_4_
  1787.4 17.8 down_part.15
  1805.2 7.8 collective-permute-start.41
  1815.0 10.2 mix_cols.7
  1826.6 18.1 down_part.16
  1844.7 6.5 collective-permute-start.42
  1851.4 18.0 down_part.17
  1876.5 8.3 mix_cols.8
  1891.4 8.3 mix_cols.9
  (188 shorter events, 107.2 us)
Async XLA Ops:
  57.5 233.3 %collective-permute-start = (bf16[1280,2048]{1,0:T(8,128)(2,1)}, bf16[1280,2048]{1,0:T(8,128)(2,1)}, u32[]{:S(2)}, u32[]{:S(2)}) collective-permute-start(bf16[1280,2048]{1,0:T(8,128)(2,1)} %get-tuple-element.95), channel_id=1, source_target_pairs={{0,1},{1,2},{2,3},{3,0},{4,5},{5,6},{6,7},{7,4}} | collective-permute-start | bytes 15728648 | tf_op jit(solution)/shard_map/ppermute | solution.py:494
  57.5 233.3 %collective-permute-start.1 = (bf16[1280,2048]{1,0:T(8,128)(2,1)}, bf16[1280,2048]{1,0:T(8,128)(2,1)}, u32[]{:S(2)}, u32[]{:S(2)}) collective-permute-start(bf16[1280,2048]{1,0:T(8,128)(2,1)} %get-tuple-element.96), channel_id=1, source_target_pairs={{0,2},{1,3},{2,0},{3,1},{4,6},{5,7},{6,4},{7,5}} | collective-permute-start | bytes 15728648 | tf_op jit(solution)/shard_map/ppermute | solution.py:494
  59.5 231.3 %collective-permute-start.2 = (bf16[1280,2048]{1,0:T(8,128)(2,1)}, bf16[1280,2048]{1,0:T(8,128)(2,1)}, u32[]{:S(2)}, u32[]{:S(2)}) collective-permute-start(bf16[1280,2048]{1,0:T(8,128)(2,1)} %get-tuple-element.97), channel_id=1, source_target_pairs={{0,3},{1,0},{2,1},{3,2},{4,7},{5,4},{6,5},{7,6}} | collective-permute-start | bytes 15728648 | tf_op jit(solution)/shard_map/ppermute | solution.py:494
  63.3 104.2 %collective-permute-start.3 = (bf16[1024,512]{1,0:T(8,128)(2,1)}, bf16[1024,512]{1,0:T(8,128)(2,1)}, u32[]{:S(2)}, u32[]{:S(2)}) collective-permute-start(bf16[1024,512]{1,0:T(8,128)(2,1)} %slice_bitcast_fusion.1), channel_id=1, source_target_pairs={{0,4},{4,0},{1,5},{5,1},{2,6},{6,2},{3,7},{7,3}} | collective-permute-start | bytes 3145736 | tf_op jit(solution)/shard_map/ppermute | solution.py:489
  84.0 370.4 %collective-permute-start.9 = (bf16[2,1024,2048]{2,1,0:T(8,128)(2,1)}, bf16[2,1024,2048]{2,1,0:T(8,128)(2,1)}, u32[]{:S(2)}, u32[]{:S(2)}) collective-permute-start(bf16[2,1024,2048]{2,1,0:T(8,128)(2,1)} %pad_maximum_fusion.1), channel_id=1, source_target_pairs={{0,4},{4,0},{1,5},{5,1},{2,6},{6,2},{3,7},{7,3}} | collective-permute-start | bytes 25165832 | tf_op jit(solution)/shard_map/ppermute | solution.py:489
  167.5 122.4 %collective-permute-start.4 = (bf16[1024,512]{1,0:T(8,128)(2,1)}, bf16[1024,512]{1,0:T(8,128)(2,1)}, u32[]{:S(2)}, u32[]{:S(2)}) collective-permute-start(bf16[1024,512]{1,0:T(8,128)(2,1)} %slice_bitcast_fusion), channel_id=1, source_target_pairs={{0,4},{4,0},{1,5},{5,1},{2,6},{6,2},{3,7},{7,3}} | collective-permute-start | bytes 3145736 | tf_op jit(solution)/shard_map/ppermute | solution.py:489
  289.9 163.7 %collective-permute-start.13 = (bf16[2,1024,1536]{2,1,0:T(8,128)(2,1)}, bf16[2,1024,1536]{2,1,0:T(8,128)(2,1)}, u32[]{:S(2)}, u32[]{:S(2)}) collective-permute-start(bf16[2,1024,1536]{2,1,0:T(8,128)(2,1)} %pad_maximum_fusion.5), channel_id=1, source_target_pairs={{0,4},{4,0},{1,5},{5,1},{2,6},{6,2},{3,7},{7,3}} | collective-permute-start | bytes 18874376 | tf_op jit(solution)/shard_map/ppermute | solution.py:489
  312.8 113.1 %collective-permute-start.5 = (s32[4,2]{0,1:T(2,128)S(1)}, s32[4,2]{0,1:T(2,128)S(1)}, u32[]{:S(2)}, u32[]{:S(2)}) collective-permute-start(s32[4,2]{0,1:T(2,128)S(1)} %select_reduce_fusion.4), channel_id=1, source_target_pairs={{0,4},{4,0},{1,5},{5,1},{2,6},{6,2},{3,7},{7,3}} | collective-permute-start | bytes 104 | tf_op jit(solution)/shard_map/ppermute | solution.py:525
  312.9 513.1 %collective-permute-start.6 = (bf16[1280,2048]{1,0:T(8,128)(2,1)}, bf16[1280,2048]{1,0:T(8,128)(2,1)}, u32[]{:S(2)}, u32[]{:S(2)}) collective-permute-start(bf16[1280,2048]{1,0:T(8,128)(2,1)} %get-tuple-element.101), channel_id=1, source_target_pairs={{0,1},{1,2},{2,3},{3,0},{4,5},{5,6},{6,7},{7,4}} | collective-permute-start | bytes 15728648 | tf_op jit(solution)/shard_map/ppermute | solution.py:494
  312.9 533.0 %collective-permute-start.7 = (bf16[1280,2048]{1,0:T(8,128)(2,1)}, bf16[1280,2048]{1,0:T(8,128)(2,1)}, u32[]{:S(2)}, u32[]{:S(2)}) collective-permute-start(bf16[1280,2048]{1,0:T(8,128)(2,1)} %get-tuple-element.103), channel_id=1, source_target_pairs={{0,2},{1,3},{2,0},{3,1},{4,6},{5,7},{6,4},{7,5}} | collective-permute-start | bytes 15728648 | tf_op jit(solution)/shard_map/ppermute | solution.py:494
  425.9 421.6 %collective-permute-start.8 = (bf16[1280,2048]{1,0:T(8,128)(2,1)}, bf16[1280,2048]{1,0:T(8,128)(2,1)}, u32[]{:S(2)}, u32[]{:S(2)}) collective-permute-start(bf16[1280,2048]{1,0:T(8,128)(2,1)} %get-tuple-element.105), channel_id=1, source_target_pairs={{0,3},{1,0},{2,1},{3,2},{4,7},{5,4},{6,5},{7,6}} | collective-permute-start | bytes 15728648 | tf_op jit(solution)/shard_map/ppermute | solution.py:494
  453.6 81.1 %collective-permute-start.14 = (bf16[2,1024,512]{2,1,0:T(8,128)(2,1)}, bf16[2,1024,512]{2,1,0:T(8,128)(2,1)}, u32[]{:S(2)}, u32[]{:S(2)}) collective-permute-start(bf16[2,1024,512]{2,1,0:T(8,128)(2,1)} %pad_maximum_fusion.6), channel_id=1, source_target_pairs={{0,4},{4,0},{1,5},{5,1},{2,6},{6,2},{3,7},{7,3}} | collective-permute-start | bytes 6291464 | tf_op jit(solution)/shard_map/ppermute | solution.py:489
  454.4 182.9 %collective-permute-start.10 = (bf16[2,1024,1536]{2,1,0:T(8,128)(2,1)}, bf16[2,1024,1536]{2,1,0:T(8,128)(2,1)}, u32[]{:S(2)}, u32[]{:S(2)}) collective-permute-start(bf16[2,1024,1536]{2,1,0:T(8,128)(2,1)} %pad_maximum_fusion.3), channel_id=1, source_target_pairs={{0,4},{4,0},{1,5},{5,1},{2,6},{6,2},{3,7},{7,3}} | collective-permute-start | bytes 18874376 | tf_op jit(solution)/shard_map/ppermute | solution.py:489
  534.7 237.3 %collective-permute-start.15 = (bf16[2,1024,1536]{2,1,0:T(8,128)(2,1)}, bf16[2,1024,1536]{2,1,0:T(8,128)(2,1)}, u32[]{:S(2)}, u32[]{:S(2)}) collective-permute-start(bf16[2,1024,1536]{2,1,0:T(8,128)(2,1)} %pad_maximum_fusion.4), channel_id=1, source_target_pairs={{0,4},{4,0},{1,5},{5,1},{2,6},{6,2},{3,7},{7,3}} | collective-permute-start | bytes 18874376 | tf_op jit(solution)/shard_map/ppermute | solution.py:489
  637.3 438.5 %collective-permute-start.11 = (bf16[2,1024,2048]{2,1,0:T(8,128)(2,1)}, bf16[2,1024,2048]{2,1,0:T(8,128)(2,1)}, u32[]{:S(2)}, u32[]{:S(2)}) collective-permute-start(bf16[2,1024,2048]{2,1,0:T(8,128)(2,1)} %pad_maximum_fusion), channel_id=1, source_target_pairs={{0,4},{4,0},{1,5},{5,1},{2,6},{6,2},{3,7},{7,3}} | collective-permute-start | bytes 25165832 | tf_op jit(solution)/shard_map/ppermute | solution.py:489
  772.1 302.5 %collective-permute-start.16 = (bf16[5632,512]{1,0:T(8,128)(2,1)}, bf16[5632,512]{1,0:T(8,128)(2,1)}, u32[]{:S(2)}, u32[]{:S(2)}) collective-permute-start(bf16[5632,512]{1,0:T(8,128)(2,1)} %get-tuple-element.118), channel_id=1, source_target_pairs={{0,4},{4,0},{1,5},{5,1},{2,6},{6,2},{3,7},{7,3}} | collective-permute-start | bytes 17301512 | tf_op jit(solution)/shard_map/ppermute | solution.py:489
  825.9 705.5 %collective-permute-start.18 = (bf16[1280,1024]{1,0:T(8,128)(2,1)}, bf16[1280,1024]{1,0:T(8,128)(2,1)}, u32[]{:S(2)}, u32[]{:S(2)}) collective-permute-start(bf16[1280,1024]{1,0:T(8,128)(2,1)} %get-tuple-element.124), channel_id=1, source_target_pairs={{0,3},{1,0},{2,1},{3,2},{4,7},{5,4},{6,5},{7,6}} | collective-permute-start | bytes 7864328 | tf_op jit(solution)/shard_map/ppermute | solution.py:494
  845.9 715.5 %collective-permute-start.20 = (bf16[1280,1024]{1,0:T(8,128)(2,1)}, bf16[1280,1024]{1,0:T(8,128)(2,1)}, u32[]{:S(2)}, u32[]{:S(2)}) collective-permute-start(bf16[1280,1024]{1,0:T(8,128)(2,1)} %get-tuple-element.126), channel_id=1, source_target_pairs={{0,2},{1,3},{2,0},{3,1},{4,6},{5,7},{6,4},{7,5}} | collective-permute-start | bytes 7864328 | tf_op jit(solution)/shard_map/ppermute | solution.py:494
  847.5 724.8 %collective-permute-start.22 = (bf16[1280,1024]{1,0:T(8,128)(2,1)}, bf16[1280,1024]{1,0:T(8,128)(2,1)}, u32[]{:S(2)}, u32[]{:S(2)}) collective-permute-start(bf16[1280,1024]{1,0:T(8,128)(2,1)} %get-tuple-element.128), channel_id=1, source_target_pairs={{0,1},{1,2},{2,3},{3,0},{4,5},{5,6},{6,7},{7,4}} | collective-permute-start | bytes 7864328 | tf_op jit(solution)/shard_map/ppermute | solution.py:494
  1074.6 81.2 %collective-permute-start.24 = (bf16[5632,256]{1,0:T(8,128)(2,1)}, bf16[5632,256]{1,0:T(8,128)(2,1)}, u32[]{:S(2)}, u32[]{:S(2)}) collective-permute-start(bf16[5632,256]{1,0:T(8,128)(2,1)} %get-tuple-element.131), channel_id=1, source_target_pairs={{0,4},{4,0},{1,5},{5,1},{2,6},{6,2},{3,7},{7,3}} | collective-permute-start | bytes 8650760 | tf_op jit(solution)/shard_map/ppermute | solution.py:489
  1075.8 259.4 %collective-permute-start.12 = (bf16[2,1024,1536]{2,1,0:T(8,128)(2,1)}, bf16[2,1024,1536]{2,1,0:T(8,128)(2,1)}, u32[]{:S(2)}, u32[]{:S(2)}) collective-permute-start(bf16[2,1024,1536]{2,1,0:T(8,128)(2,1)} %pad_maximum_fusion.2), channel_id=1, source_target_pairs={{0,4},{4,0},{1,5},{5,1},{2,6},{6,2},{3,7},{7,3}} | collective-permute-start | bytes 18874376 | tf_op jit(solution)/shard_map/ppermute | solution.py:489
  1155.8 179.4 %collective-permute-start.32 = (bf16[5632,256]{1,0:T(8,128)(2,1)}, bf16[5632,256]{1,0:T(8,128)(2,1)}, u32[]{:S(2)}, u32[]{:S(2)}) collective-permute-start(bf16[5632,256]{1,0:T(8,128)(2,1)} %get-tuple-element.145), channel_id=1, source_target_pairs={{0,4},{4,0},{1,5},{5,1},{2,6},{6,2},{3,7},{7,3}} | collective-permute-start | bytes 8650760 | tf_op jit(solution)/shard_map/ppermute | solution.py:489
  1335.2 196.3 %collective-permute-start.17 = (bf16[5632,512]{1,0:T(8,128)(2,1)}, bf16[5632,512]{1,0:T(8,128)(2,1)}, u32[]{:S(2)}, u32[]{:S(2)}) collective-permute-start(bf16[5632,512]{1,0:T(8,128)(2,1)} %get-tuple-element.121), channel_id=1, source_target_pairs={{0,4},{4,0},{1,5},{5,1},{2,6},{6,2},{3,7},{7,3}} | collective-permute-start | bytes 17301512 | tf_op jit(solution)/shard_map/ppermute | solution.py:489
  1478.4 110.6 %collective-permute-start.19 = (bf16[1280,1024]{1,0:T(8,128)(2,1)}, bf16[1280,1024]{1,0:T(8,128)(2,1)}, u32[]{:S(2)}, u32[]{:S(2)}) collective-permute-start(bf16[1280,1024]{1,0:T(8,128)(2,1)} %get-tuple-element.125), channel_id=1, source_target_pairs={{0,3},{1,0},{2,1},{3,2},{4,7},{5,4},{6,5},{7,6}} | collective-permute-start | bytes 7864328 | tf_op jit(solution)/shard_map/ppermute | solution.py:494
  1531.4 113.7 %collective-permute-start.21 = (bf16[1280,1024]{1,0:T(8,128)(2,1)}, bf16[1280,1024]{1,0:T(8,128)(2,1)}, u32[]{:S(2)}, u32[]{:S(2)}) collective-permute-start(bf16[1280,1024]{1,0:T(8,128)(2,1)} %get-tuple-element.127), channel_id=1, source_target_pairs={{0,2},{1,3},{2,0},{3,1},{4,6},{5,7},{6,4},{7,5}} | collective-permute-start | bytes 7864328 | tf_op jit(solution)/shard_map/ppermute | solution.py:494
  1531.4 115.5 %collective-permute-start.23 = (bf16[1280,1024]{1,0:T(8,128)(2,1)}, bf16[1280,1024]{1,0:T(8,128)(2,1)}, u32[]{:S(2)}, u32[]{:S(2)}) collective-permute-start(bf16[1280,1024]{1,0:T(8,128)(2,1)} %get-tuple-element.129), channel_id=1, source_target_pairs={{0,1},{1,2},{2,3},{3,0},{4,5},{5,6},{6,7},{7,4}} | collective-permute-start | bytes 7864328 | tf_op jit(solution)/shard_map/ppermute | solution.py:494
  1561.5 132.0 %collective-permute-start.26 = (bf16[1280,512]{1,0:T(8,128)(2,1)}, bf16[1280,512]{1,0:T(8,128)(2,1)}, u32[]{:S(2)}, u32[]{:S(2)}) collective-permute-start(bf16[1280,512]{1,0:T(8,128)(2,1)} %get-tuple-element.137), channel_id=1, source_target_pairs={{0,3},{1,0},{2,1},{3,2},{4,7},{5,4},{6,5},{7,6}} | collective-permute-start | bytes 3932168 | tf_op jit(solution)/shard_map/ppermute | solution.py:494
  1572.3 147.2 %collective-permute-start.28 = (bf16[1280,512]{1,0:T(8,128)(2,1)}, bf16[1280,512]{1,0:T(8,128)(2,1)}, u32[]{:S(2)}, u32[]{:S(2)}) collective-permute-start(bf16[1280,512]{1,0:T(8,128)(2,1)} %get-tuple-element.139), channel_id=1, source_target_pairs={{0,2},{1,3},{2,0},{3,1},{4,6},{5,7},{6,4},{7,5}} | collective-permute-start | bytes 3932168 | tf_op jit(solution)/shard_map/ppermute | solution.py:494
  1589.0 130.5 %collective-permute-start.30 = (bf16[1280,512]{1,0:T(8,128)(2,1)}, bf16[1280,512]{1,0:T(8,128)(2,1)}, u32[]{:S(2)}, u32[]{:S(2)}) collective-permute-start(bf16[1280,512]{1,0:T(8,128)(2,1)} %get-tuple-element.141), channel_id=1, source_target_pairs={{0,1},{1,2},{2,3},{3,0},{4,5},{5,6},{6,7},{7,4}} | collective-permute-start | bytes 3932168 | tf_op jit(solution)/shard_map/ppermute | solution.py:494
  1645.2 55.4 %collective-permute-start.25 = (bf16[5632,256]{1,0:T(8,128)(2,1)}, bf16[5632,256]{1,0:T(8,128)(2,1)}, u32[]{:S(2)}, u32[]{:S(2)}) collective-permute-start(bf16[5632,256]{1,0:T(8,128)(2,1)} %get-tuple-element.134), channel_id=1, source_target_pairs={{0,4},{4,0},{1,5},{5,1},{2,6},{6,2},{3,7},{7,3}} | collective-permute-start | bytes 8650760 | tf_op jit(solution)/shard_map/ppermute | solution.py:489
  1691.6 36.6 %collective-permute-start.27 = (bf16[1280,512]{1,0:T(8,128)(2,1)}, bf16[1280,512]{1,0:T(8,128)(2,1)}, u32[]{:S(2)}, u32[]{:S(2)}) collective-permute-start(bf16[1280,512]{1,0:T(8,128)(2,1)} %get-tuple-element.138), channel_id=1, source_target_pairs={{0,3},{1,0},{2,1},{3,2},{4,7},{5,4},{6,5},{7,6}} | collective-permute-start | bytes 3932168 | tf_op jit(solution)/shard_map/ppermute | solution.py:494
  1693.5 65.1 %collective-permute-start.29 = (bf16[1280,512]{1,0:T(8,128)(2,1)}, bf16[1280,512]{1,0:T(8,128)(2,1)}, u32[]{:S(2)}, u32[]{:S(2)}) collective-permute-start(bf16[1280,512]{1,0:T(8,128)(2,1)} %get-tuple-element.140), channel_id=1, source_target_pairs={{0,2},{1,3},{2,0},{3,1},{4,6},{5,7},{6,4},{7,5}} | collective-permute-start | bytes 3932168 | tf_op jit(solution)/shard_map/ppermute | solution.py:494
  1700.6 58.0 %collective-permute-start.31 = (bf16[1280,512]{1,0:T(8,128)(2,1)}, bf16[1280,512]{1,0:T(8,128)(2,1)}, u32[]{:S(2)}, u32[]{:S(2)}) collective-permute-start(bf16[1280,512]{1,0:T(8,128)(2,1)} %get-tuple-element.142), channel_id=1, source_target_pairs={{0,1},{1,2},{2,3},{3,0},{4,5},{5,6},{6,7},{7,4}} | collective-permute-start | bytes 3932168 | tf_op jit(solution)/shard_map/ppermute | solution.py:494
  1719.4 131.8 %collective-permute-start.40 = (bf16[5632,128]{1,0:T(8,128)(2,1)}, bf16[5632,128]{1,0:T(8,128)(2,1)}, u32[]{:S(2)}, u32[]{:S(2)}) collective-permute-start(bf16[5632,128]{1,0:T(8,128)(2,1)} %get-tuple-element.159), channel_id=1, source_target_pairs={{0,4},{4,0},{1,5},{5,1},{2,6},{6,2},{3,7},{7,3}} | collective-permute-start | bytes 4325384 | tf_op jit(solution)/shard_map/ppermute | solution.py:489
  1719.5 58.5 %collective-permute-start.33 = (bf16[1280,256]{1,0:T(8,128)(2,1)}, bf16[1280,256]{1,0:T(8,128)(2,1)S(1)}, u32[]{:S(2)}, u32[]{:S(2)}) collective-permute-start(bf16[1280,256]{1,0:T(8,128)(2,1)} %get-tuple-element.148), channel_id=1, source_target_pairs={{0,3},{1,0},{2,1},{3,2},{4,7},{5,4},{6,5},{7,6}} | collective-permute-start | bytes 1966088 | tf_op jit(solution)/shard_map/ppermute | solution.py:494
  1728.3 58.4 %collective-permute-start.35 = (bf16[1280,256]{1,0:T(8,128)(2,1)}, bf16[1280,256]{1,0:T(8,128)(2,1)}, u32[]{:S(2)}, u32[]{:S(2)}) collective-permute-start(bf16[1280,256]{1,0:T(8,128)(2,1)} %get-tuple-element.150), channel_id=1, source_target_pairs={{0,2},{1,3},{2,0},{3,1},{4,6},{5,7},{6,4},{7,5}} | collective-permute-start | bytes 1966088 | tf_op jit(solution)/shard_map/ppermute | solution.py:494
  1758.6 28.1 %collective-permute-start.37 = (bf16[1280,256]{1,0:T(8,128)(2,1)}, bf16[1280,256]{1,0:T(8,128)(2,1)}, u32[]{:S(2)}, u32[]{:S(2)}) collective-permute-start(bf16[1280,256]{1,0:T(8,128)(2,1)} %get-tuple-element.152), channel_id=1, source_target_pairs={{0,1},{1,2},{2,3},{3,0},{4,5},{5,6},{6,7},{7,4}} | collective-permute-start | bytes 1966088 | tf_op jit(solution)/shard_map/ppermute | solution.py:494
  1758.6 46.7 %collective-permute-start.34 = (bf16[1280,256]{1,0:T(8,128)(2,1)}, bf16[1280,256]{1,0:T(8,128)(2,1)}, u32[]{:S(2)}, u32[]{:S(2)}) collective-permute-start(bf16[1280,256]{1,0:T(8,128)(2,1)} %get-tuple-element.149), channel_id=1, source_target_pairs={{0,3},{1,0},{2,1},{3,2},{4,7},{5,4},{6,5},{7,6}} | collective-permute-start | bytes 1966088 | tf_op jit(solution)/shard_map/ppermute | solution.py:494
  1778.0 36.5 %collective-permute-start.36 = (bf16[1280,256]{1,0:T(8,128)(2,1)}, bf16[1280,256]{1,0:T(8,128)(2,1)}, u32[]{:S(2)}, u32[]{:S(2)}) collective-permute-start(bf16[1280,256]{1,0:T(8,128)(2,1)} %get-tuple-element.151), channel_id=1, source_target_pairs={{0,2},{1,3},{2,0},{3,1},{4,6},{5,7},{6,4},{7,5}} | collective-permute-start | bytes 1966088 | tf_op jit(solution)/shard_map/ppermute | solution.py:494
  1786.6 28.4 %collective-permute-start.38 = (bf16[1280,256]{1,0:T(8,128)(2,1)}, bf16[1280,256]{1,0:T(8,128)(2,1)}, u32[]{:S(2)}, u32[]{:S(2)}) collective-permute-start(bf16[1280,256]{1,0:T(8,128)(2,1)} %get-tuple-element.153), channel_id=1, source_target_pairs={{0,1},{1,2},{2,3},{3,0},{4,5},{5,6},{6,7},{7,4}} | collective-permute-start | bytes 1966088 | tf_op jit(solution)/shard_map/ppermute | solution.py:494
  1786.6 39.9 %collective-permute-start.39 = (bf16[5632,128]{1,0:T(8,128)(2,1)}, bf16[5632,128]{1,0:T(8,128)(2,1)}, u32[]{:S(2)}, u32[]{:S(2)}) collective-permute-start(bf16[5632,128]{1,0:T(8,128)(2,1)} %get-tuple-element.156), channel_id=1, source_target_pairs={{0,4},{4,0},{1,5},{5,1},{2,6},{6,2},{3,7},{7,3}} | collective-permute-start | bytes 4325384 | tf_op jit(solution)/shard_map/ppermute | solution.py:489
  1805.2 46.0 %collective-permute-start.41 = (bf16[1280,256]{1,0:T(8,128)(2,1)}, bf16[1280,256]{1,0:T(8,128)(2,1)S(1)}, u32[]{:S(2)}, u32[]{:S(2)}) collective-permute-start(bf16[1280,256]{1,0:T(8,128)(2,1)} %get-tuple-element.162), channel_id=1, source_target_pairs={{0,3},{1,0},{2,1},{3,2},{4,7},{5,4},{6,5},{7,6}} | collective-permute-start | bytes 1966088 | tf_op jit(solution)/shard_map/ppermute | solution.py:494
  1814.6 54.9 %collective-permute-start.43 = (bf16[1280,256]{1,0:T(8,128)(2,1)}, bf16[1280,256]{1,0:T(8,128)(2,1)}, u32[]{:S(2)}, u32[]{:S(2)}) collective-permute-start(bf16[1280,256]{1,0:T(8,128)(2,1)} %get-tuple-element.164), channel_id=1, source_target_pairs={{0,2},{1,3},{2,0},{3,1},{4,6},{5,7},{6,4},{7,5}} | collective-permute-start | bytes 1966088 | tf_op jit(solution)/shard_map/ppermute | solution.py:494
  1815.0 60.7 %collective-permute-start.45 = (bf16[1280,256]{1,0:T(8,128)(2,1)}, bf16[1280,256]{1,0:T(8,128)(2,1)}, u32[]{:S(2)}, u32[]{:S(2)}) collective-permute-start(bf16[1280,256]{1,0:T(8,128)(2,1)} %get-tuple-element.166), channel_id=1, source_target_pairs={{0,1},{1,2},{2,3},{3,0},{4,5},{5,6},{6,7},{7,4}} | collective-permute-start | bytes 1966088 | tf_op jit(solution)/shard_map/ppermute | solution.py:494
  1844.7 31.1 %collective-permute-start.42 = (bf16[1280,128]{1,0:T(8,128)(2,1)}, bf16[1280,128]{1,0:T(8,128)(2,1)S(1)}, u32[]{:S(2)}, u32[]{:S(2)}) collective-permute-start(bf16[1280,128]{1,0:T(8,128)(2,1)} %get-tuple-element.163), channel_id=1, source_target_pairs={{0,3},{1,0},{2,1},{3,2},{4,7},{5,4},{6,5},{7,6}} | collective-permute-start | bytes 983048 | tf_op jit(solution)/shard_map/ppermute | solution.py:494
  1851.2 24.7 %collective-permute-start.44 = (bf16[1280,128]{1,0:T(8,128)(2,1)}, bf16[1280,128]{1,0:T(8,128)(2,1)}, u32[]{:S(2)}, u32[]{:S(2)}) collective-permute-start(bf16[1280,128]{1,0:T(8,128)(2,1)} %get-tuple-element.165), channel_id=1, source_target_pairs={{0,2},{1,3},{2,0},{3,1},{4,6},{5,7},{6,4},{7,5}} | collective-permute-start | bytes 983048 | tf_op jit(solution)/shard_map/ppermute | solution.py:494
  1851.2 24.7 %collective-permute-start.46 = (bf16[1280,128]{1,0:T(8,128)(2,1)}, bf16[1280,128]{1,0:T(8,128)(2,1)}, u32[]{:S(2)}, u32[]{:S(2)}) collective-permute-start(bf16[1280,128]{1,0:T(8,128)(2,1)} %get-tuple-element.167), channel_id=1, source_target_pairs={{0,1},{1,2},{2,3},{3,0},{4,5},{5,6},{6,7},{7,4}} | collective-permute-start | bytes 983048 | tf_op jit(solution)/shard_map/ppermute | solution.py:494
  1869.4 16.0 collective-permute-start.47
  (17 other events, 235.9 us)
